TPU v7x, 32 devices: a whole 2x2x4 slice. The times are simulated.
32 devices in a mesh: mode: 8 (over z, y), atom: 4 (over x, core).
Axes of the slice: x: 2, y: 2, z: 4, core: 2. Of those that a mesh axis runs over, the one named last changes fastest.
Arguments:
- vectors: bfloat16 [15360, 1024], P('atom', 'mode'), may hold values from -0.046875 to 0.046875
- couplings: float32 [4, 3, 3, 3, 5120], P(None, None, None, None, 'atom'), may hold values from -6 to 6, as said below
- neighbours: int32 [4, 5120], P(None, 'atom'), may hold values from 0 to 5119, as said below
- frequency: float32 [1024], replicated, may hold values from 1 to 2, as said below
Outputs:
- diffusivity: float32 [1024], P('mode')
Inputs may be any that keep to these rules, and one draw needn't show every extreme that they name: neighbours[k, i] differs from i by 2 to 64 positions in atom order, counted around the end, upward for k < 2 and downward otherwise; the lists are mutual: neighbours[k + 2, neighbours[k, i]] = i for k < 2; some atoms in every slab have a neighbour exactly 64 positions above and some exactly 64 below. Antisymmetric bonds: couplings[k + 2, a, q, p, j] = -couplings[k, a, p, q, neighbours[k + 2, j]] for k < 2. `frequency`: strictly ascending.
All inputs are finite; a program needn't handle non-finite values.
Results may differ from a plain program's by a relative error of at most 0.00075.
Values may be sent and summed in bfloat16 or wider, within the bound.
A program may use at most 128 MiB of HBM per device.

v0:
```python
import functools
import math

import jax
import jax.numpy as jnp
from jax import lax
from jax.experimental import pallas as pl
from jax.experimental.pallas import tpu as pltpu
from jax.sharding import PartitionSpec as P

HALO = 64
PARTNERS = 4
WIDTH_MODES = 320
TILE = 128
WIDE = 3 * TILE
EDGE = 3 * HALO
PERIOD = 48
SLOTS = 4
MESH = pl.DeviceIdType.MESH
BF16 = jnp.bfloat16
F32 = jnp.float32

SELF_PAIRS = ((0, 0), (1, 0), (1, 1))
NEXT_PAIRS = tuple((c, b) for c in range(2) for b in range(2) if 2 + b - c <= PARTNERS)
SKIP_PAIRS = tuple((c, b) for c in range(2) for b in range(2) if 4 + c - b <= PARTNERS)
PAIRS = len(SELF_PAIRS) + len(NEXT_PAIRS) + len(SKIP_PAIRS)


def aligned(value):
    return pl.multiple_of(value, 16)


def band_groups(lane_tile):
    first = (TILE * lane_tile) // 3
    last = (TILE * lane_tile + TILE - 1) // 3
    down = range((3 * first) // PERIOD, (3 * (last + HALO - 2) + 2) // PERIOD + 1)
    up = range((3 * (HALO + first + 2)) // PERIOD, (3 * (2 * HALO + last) + 2) // PERIOD + 1)
    return down, up


def kernel(
    sizes,
    vec,
    planes_ref,
    freq_ref,
    out_ref,
    own,
    up,
    dn,
    own_t,
    up_t,
    weights,
    spread,
    expand,
    eye,
    mixed,
    pattern,
    app_own,
    app_up,
    acc_next,
    acc_skip,
    red,
    red_in,
    given,
    taken,
    local_sem,
    y_sem,
    z_sem,
    edge_sem,
    side_sem,
    red_sem,
    fin_sem,
):
    blocks_all, groups, rows_dev, modes, half_width = sizes
    rows = rows_dev // 2
    tiles = rows // WIDE
    padded = rows + 2 * EDGE
    owners = 2 * groups
    share = modes // owners

    mode = lax.axis_index("mode")
    atom = lax.axis_index("atom")
    s = mode // 2
    y = mode % 2
    other = 1 - y
    mate = mode + 1 - 2 * y
    h = (y + atom) % 2
    supers = blocks_all // 2
    has_up = s < supers - 1
    has_dn = s > 0
    outer = (atom + 2 * h - 1 + groups) % groups
    across = (atom + 1 - 2 * h + groups) % groups

    def remote(src, dst, sems, at, device):
        return pltpu.make_async_remote_copy(
            src_ref=src,
            dst_ref=dst,
            send_sem=sems.at[(0,) + at],
            recv_sem=sems.at[(1,) + at],
            device_id=device,
            device_id_type=MESH,
        )

    barrier = pltpu.get_barrier_semaphore()

    def greet(delta):
        for side in range(2):
            for slab in range(groups):
                target = (2 * (s + delta) + side, slab)
                if delta:
                    pl.semaphore_signal(barrier, inc=1, device_id=target, device_id_type=MESH)
                else:

                    @pl.when(jnp.logical_or(side != y, slab != atom))
                    def _():
                        pl.semaphore_signal(barrier, inc=1, device_id=target, device_id_type=MESH)

    greet(0)
    pl.when(has_up)(functools.partial(greet, 1))
    pl.when(has_dn)(functools.partial(greet, -1))
    sides = has_up.astype(jnp.int32) + has_dn.astype(jnp.int32)
    pl.semaphore_wait(barrier, owners - 1 + owners * sides)

    def local_copy():
        size = rows + EDGE
        return pltpu.make_async_copy(
            vec.at[pl.ds(aligned(h * (rows - EDGE)), size), :],
            own.at[y, pl.ds(aligned((1 - h) * EDGE), size), :],
            local_sem.at[0],
        )

    def y_copy(t):
        return remote(
            vec.at[pl.ds(aligned((1 - h) * rows + t * WIDE), WIDE), :],
            own.at[y, pl.ds(aligned(EDGE + t * WIDE), WIDE), :],
            y_sem,
            (t,),
            (mate, atom),
        )

    def y_edge():
        return remote(
            vec.at[pl.ds(aligned(rows - EDGE + h * EDGE), EDGE), :],
            own.at[y, pl.ds(aligned(h * (rows + EDGE)), EDGE), :],
            edge_sem,
            (0,),
            (mate, atom),
        )

    def outer_edge():
        return remote(
            vec.at[pl.ds(aligned(h * (rows_dev - EDGE)), EDGE), :],
            own.at[y, pl.ds(aligned((1 - h) * (rows + EDGE)), EDGE), :],
            edge_sem,
            (1,),
            (mode, outer),
        )

    def across_edge():
        return remote(
            vec.at[pl.ds(aligned((1 - h) * (rows_dev - EDGE)), EDGE), :],
            own.at[y, pl.ds(aligned(h * (rows + EDGE)), EDGE), :],
            edge_sem,
            (2,),
            (mate, across),
        )

    def z_copy(upward, relay, t):
        if relay:
            src = own.at[other, pl.ds(aligned(EDGE + t * WIDE), WIDE), :]
            place = other
        else:
            src = vec.at[pl.ds(aligned(h * rows + t * WIDE), WIDE), :]
            place = y
        if upward:
            dst = dn.at[place, pl.ds(aligned(t * WIDE), WIDE), :]
            return remote(src, dst, z_sem, (0, relay, t), (mode + 2, atom))
        dst = up.at[place, pl.ds(aligned(EDGE + t * WIDE), WIDE), :]
        return remote(src, dst, z_sem, (1, relay, t), (mode - 2, atom))

    def side_copy(inner):
        if inner:
            src = EDGE + (1 - h) * (rows - EDGE)
            dst = h * (rows + EDGE)
            device = (mate, atom)
        else:
            src = EDGE + h * (rows - EDGE)
            dst = (1 - h) * (rows + EDGE)
            device = (mode, outer)
        return remote(
            up.at[:, pl.ds(aligned(src), EDGE), :],
            up.at[:, pl.ds(aligned(dst), EDGE), :],
            side_sem,
            (inner,),
            device,
        )

    local_copy().start()
    order = [tiles - 1] + list(range(tiles - 1))
    for t in order:
        y_copy(t).start()

        @pl.when(has_up)
        def _():
            z_copy(1, 0, t).start()

        @pl.when(has_dn)
        def _():
            z_copy(0, 0, t).start()

    y_edge().start()
    outer_edge().start()
    across_edge().start()

    @pl.when(jnp.logical_not(has_dn))
    def _():
        taken[0:owners] = jnp.zeros((owners, 8, modes), F32)

    @pl.when(jnp.logical_not(has_up))
    def _():
        taken[2 * owners : 3 * owners] = jnp.zeros((owners, 8, modes), F32)

    row = lax.broadcasted_iota(jnp.int32, (WIDE, WIDE), 0)
    col = lax.broadcasted_iota(jnp.int32, (WIDE, WIDE), 1)
    spread[...] = jnp.where(col == 3 * (row % TILE) + row // TILE, 1.0, 0.0).astype(BF16)
    row = lax.broadcasted_iota(jnp.int32, (TILE, TILE), 0)
    col = lax.broadcasted_iota(jnp.int32, (TILE, TILE), 1)
    eye[...] = jnp.where(row == col, 1.0, 0.0).astype(BF16)
    height = 3 * SLOTS * PERIOD
    row = lax.broadcasted_iota(jnp.int32, (height + 16 * SLOTS, PERIOD), 0)
    col = lax.broadcasted_iota(jnp.int32, (height + 16 * SLOTS, PERIOD), 1)
    value_col = 3 * (row // PERIOD) + (row % PERIOD) % 3
    place_col = 9 * SLOTS + (row - height) // 16
    want = jnp.where(row < height, value_col, place_col)
    expand[...] = jnp.where(col == want, 1.0, 0.0).astype(BF16)

    first_lane = h * (rows // 3)
    stacked = []
    for t in range(tiles):
        lanes = pl.ds(pl.multiple_of(first_lane + t * TILE, TILE), TILE)
        stacked.append(jnp.concatenate([planes_ref[p, :, lanes] for p in range(3)], axis=1))
    stacked = jnp.concatenate(stacked, axis=0)
    mixed[...] = (
        jnp.dot(stacked, spread[...], preferred_element_type=F32)
        .astype(BF16)
        .reshape(tiles, PERIOD, WIDE)
    )

    atom_row = (lax.broadcasted_iota(jnp.int32, (PERIOD, TILE), 0) // 3).astype(F32).astype(BF16)
    atom_row = atom_row.reshape(3, 16, TILE)

    def build(t):
        pattern[...] = jnp.dot(expand[...], mixed[t], preferred_element_type=F32).astype(BF16)
        for lane_tile in range(3):
            lanes = slice(lane_tile * TILE, (lane_tile + 1) * TILE)
            down, above = band_groups(lane_tile)
            for g in range(2 * WIDE // PERIOD):
                slots = ([0, 1] if g in above else []) + ([2, 3] if g in down else [])
                span = slice(g * PERIOD, (g + 1) * PERIOD)
                if not slots:
                    for a in range(3):
                        weights[t, a, span, lanes] = jnp.zeros((PERIOD, TILE), BF16)
                    continue
                here = atom_row + jnp.asarray(16.0 * g, BF16)
                flags = {}
                for k in slots:
                    target = pattern[height + 16 * k : height + 16 * (k + 1), lanes]
                    flags[k] = here == target[None]
                for a in range(3):
                    total = None
                    for k in slots:
                        first = (3 * k + a) * PERIOD
                        value = pattern[first : first + PERIOD, lanes].reshape(3, 16, TILE)
                        term = jnp.where(flags[k], value, jnp.zeros_like(value))
                        total = term if total is None else total + term
                    weights[t, a, span, lanes] = total.reshape(PERIOD, TILE)

    def first_phase(step, carry):
        build(step)
        t = (step + tiles - 1) % tiles
        y_copy(t).wait_recv()

        @pl.when(has_up)
        def _():
            z_copy(1, 1, t).start()

        @pl.when(has_dn)
        def _():
            z_copy(0, 1, t).start()

        return carry

    lax.fori_loop(0, tiles, first_phase, 0)

    def transposed(source, target, u):
        span = pl.ds(pl.multiple_of(u * WIDE, WIDE), WIDE)
        for j in range(2):
            target[j * modes : (j + 1) * modes, span] = lax.dot_general(
                eye[...], source[j, span, :], (((1,), (1,)), ((), ())), preferred_element_type=F32
            ).astype(BF16)

    def apply(source_t, target, t):
        window = source_t[:, pl.ds(pl.multiple_of(t * WIDE, WIDE), 2 * WIDE)]
        for a in range(3):
            target[a * 2 * modes : (a + 1) * 2 * modes, pl.ds(pl.multiple_of(t * WIDE, WIDE), WIDE)] = (
                jnp.dot(window, weights[t, a], preferred_element_type=F32).astype(BF16)
            )

    local_copy().wait()
    y_edge().wait_recv()
    outer_edge().wait_recv()
    across_edge().wait_recv()

    def own_transpose(u, carry):
        transposed(own, own_t, u)
        return carry

    lax.fori_loop(0, tiles + 1, own_transpose, 0)

    def own_apply(t, carry):
        apply(own_t, app_own, t)
        return carry

    lax.fori_loop(0, tiles, own_apply, 0)

    def store_pairs(first, pairs, a, block):
        for at, (c, b) in enumerate(pairs):
            piece = block[c * modes : (c + 1) * modes, b * modes : (b + 1) * modes]
            index = 3 * (first + at) + a
            red[:, index] = piece.astype(BF16).reshape(owners, share, modes)

    own_main = jnp.concatenate([own[j, EDGE : EDGE + rows, :] for j in range(2)], axis=1)
    for a in range(3):
        part = app_own[a * 2 * modes : (a + 1) * 2 * modes, :]
        store_pairs(0, SELF_PAIRS, a, jnp.dot(part, own_main, preferred_element_type=F32))

    def add_next(t, start):
        far = jnp.concatenate(
            [up[j, EDGE + t * WIDE : EDGE + (t + 1) * WIDE, :] for j in range(2)], axis=1
        )
        for a in range(3):
            part = slice(a * 2 * modes, (a + 1) * 2 * modes)
            term = jnp.dot(
                app_own[part, t * WIDE : (t + 1) * WIDE], far, preferred_element_type=F32
            )
            acc_next[part, :] = term if start else acc_next[part, :] + term

    def add_skip(t, start):
        far = jnp.concatenate([dn[j, t * WIDE : (t + 1) * WIDE, :] for j in range(2)], axis=1)
        for a in range(3):
            part = slice(a * 2 * modes, (a + 1) * 2 * modes)
            term = jnp.dot(
                app_up[part, t * WIDE : (t + 1) * WIDE], far, preferred_element_type=F32
            )
            acc_skip[part, :] = term if start else acc_skip[part, :] + term

    def await_chunk(t):
        for relay in range(2):

            @pl.when(has_up)
            def _():
                z_copy(0, relay, t).wait_recv()

            @pl.when(has_dn)
            def _():
                z_copy(1, relay, t).wait_recv()

    moved = set()
    applied = []
    arrived = set()
    for at, t in enumerate(order):
        await_chunk(t)
        arrived.add(t)
        if at == 1:

            @pl.when(has_up)
            def _():
                side_copy(0).start()
                side_copy(1).start()

        add_next(t, at == 0)
        if at == 2:

            @pl.when(has_up)
            def _():
                side_copy(0).wait_recv()
                side_copy(1).wait_recv()

        if at >= 2:
            for u in range(tiles + 1):
                need = {v for v in (u - 1, u) if 0 <= v < tiles}
                if u not in moved and need <= arrived:
                    transposed(up, up_t, u)
                    moved.add(u)
            for v in range(tiles):
                if v not in applied and {v, v + 1} <= moved:
                    apply(up_t, app_up, v)
                    add_skip(v, not applied)
                    applied.append(v)

    for a in range(3):
        part = slice(a * 2 * modes, (a + 1) * 2 * modes)
        store_pairs(len(SELF_PAIRS), NEXT_PAIRS, a, acc_next[part, :])
        store_pairs(len(SELF_PAIRS) + len(NEXT_PAIRS), SKIP_PAIRS, a, acc_skip[part, :])

    stages = []
    bit = 1
    while bit < groups:
        side = (atom // bit) % 2
        stages.append((side, (mode, atom + bit * (1 - 2 * side))))
        bit *= 2
    stages.append((y, (mate, atom)))
    base = 0
    size = owners
    landing = 0
    reductions = []
    for stage, (side, device) in enumerate(stages):
        size //= 2
        keep = base + side * size
        give = base + (1 - side) * size
        copy = remote(
            red.at[pl.ds(give, size)],
            red_in.at[pl.ds(landing, size)],
            red_sem,
            (stage,),
            device,
        )
        copy.start()
        copy.wait_recv()
        reductions.append(copy)
        for i in range(size):
            red[keep + i] = (
                red[keep + i].astype(F32) + red_in[landing + i].astype(F32)
            ).astype(BF16)
        landing += size
        base = keep
    mine = base

    lane = lax.broadcasted_iota(jnp.int32, (share, modes), 1)
    spot = lane == lax.broadcasted_iota(jnp.int32, (share, modes), 0) + mine * share

    def frequency(block):
        index = jnp.clip(block, 0, blocks_all - 1)
        return freq_ref[pl.ds(index, 1), :]

    def folded(value):
        return jnp.sum(value.reshape(share // 8, 8, modes), axis=0)

    sums = [jnp.zeros((8, modes), F32) for _ in range(6)]
    index = 0
    for pairs, c_base, b_base, valid in (
        (SELF_PAIRS, 2, 2, None),
        (NEXT_PAIRS, 2, 4, has_up),
        (SKIP_PAIRS, 4, 0, jnp.logical_and(has_up, has_dn)),
    ):
        for c, b in pairs:
            squares = jnp.zeros((share, modes), F32)
            for a in range(3):
                value = red[mine, 3 * index + a].astype(F32)
                squares = squares + value * value
            index += 1
            c_row = frequency(2 * s - 2 + c_base + c)
            b_row = frequency(2 * s - 2 + b_base + b)
            c_col = jnp.sum(jnp.where(spot, c_row, 0.0), axis=1, keepdims=True)
            offset = b_row - c_col
            terms = squares * (half_width / math.pi / (offset * offset + half_width * half_width))
            if valid is not None:
                terms = jnp.where(valid, terms, 0.0)
            sums[b_base + b] = sums[b_base + b] + folded(terms)
            if c_base + c != b_base + b:
                col_sum = jnp.sum(terms, axis=1, keepdims=True)
                sums[c_base + c] = sums[c_base + c] + folded(jnp.where(spot, col_sum, 0.0))
    for i in range(6):
        given[i] = sums[i]

    rank = y * groups + atom

    def final_copy(delta, side, slab):
        slot = (1 - delta) * owners + rank
        return pltpu.make_async_remote_copy(
            src_ref=given.at[2 * (delta + 1) + side],
            dst_ref=taken.at[slot],
            send_sem=fin_sem.at[0, (delta + 1) * owners + side * groups + slab],
            recv_sem=fin_sem.at[1, slot],
            device_id=(2 * (s + delta) + side, slab),
            device_id_type=MESH,
        )

    def final_wait(delta, side, slab):
        slot = (delta + 1) * owners + side * groups + slab
        return pltpu.make_async_remote_copy(
            src_ref=given.at[0],
            dst_ref=taken.at[slot],
            send_sem=fin_sem.at[0, slot],
            recv_sem=fin_sem.at[1, slot],
            device_id=(2 * (s + delta) + side, slab),
            device_id_type=MESH,
        )

    def for_all(action):
        for delta, valid in ((0, None), (1, has_up), (-1, has_dn)):
            for side in range(2):
                for slab in range(groups):
                    if valid is None:
                        condition = jnp.logical_or(side != y, slab != atom)
                    else:
                        condition = valid
                    pl.when(condition)(functools.partial(action, delta, side, slab))

    for_all(lambda *at: final_copy(*at).start())
    taken[owners + rank] = given[2 + y]
    for_all(lambda *at: final_wait(*at).wait_recv())
    total = jnp.sum(jnp.sum(taken[...], axis=0), axis=0, keepdims=True)
    own_freq = frequency(mode)
    out_ref[...] = math.pi / (3.0 * own_freq * own_freq) * total

    for_all(lambda *at: final_copy(*at).wait_send())
    for copy in reductions:
        copy.wait_send()
    y_edge().wait_send()
    outer_edge().wait_send()
    across_edge().wait_send()
    for t in range(tiles):
        y_copy(t).wait_send()

    @pl.when(has_up)
    def _():
        side_copy(0).wait_send()
        side_copy(1).wait_send()
        for relay in range(2):
            for t in range(tiles):
                z_copy(1, relay, t).wait_send()

    @pl.when(has_dn)
    def _():
        for relay in range(2):
            for t in range(tiles):
                z_copy(0, relay, t).wait_send()


def local(vectors, couplings, neighbours, frequency):
    rows_dev, modes = vectors.shape
    atoms_dev = rows_dev // 3
    blocks_all = lax.axis_size("mode")
    groups = lax.axis_size("atom")
    total_atoms = atoms_dev * groups
    half_width = WIDTH_MODES / (modes * blocks_all)
    rows = rows_dev // 2
    tiles = rows // WIDE
    padded = rows + 2 * EDGE
    owners = 2 * groups

    here = lax.axis_index("atom") * atoms_dev + jnp.arange(atoms_dev, dtype=jnp.int32)
    offset = neighbours - here[None, :]
    offset = jnp.where(offset > HALO, offset - total_atoms, offset)
    offset = jnp.where(offset < -HALO, offset + total_atoms, offset)
    window = (offset + HALO + here[None, :] % TILE).astype(BF16)
    values = couplings.transpose(2, 0, 1, 3, 4).reshape(3, 9 * SLOTS, atoms_dev).astype(BF16)
    planes = jnp.concatenate(
        [
            values,
            jnp.broadcast_to(window[None], (3, SLOTS, atoms_dev)),
            jnp.zeros((3, PERIOD - 10 * SLOTS, atoms_dev), BF16),
        ],
        axis=1,
    )
    sizes = (blocks_all, groups, rows_dev, modes, half_width)
    dma = pltpu.SemaphoreType.DMA
    result = pl.pallas_call(
        functools.partial(kernel, sizes),
        out_shape=jax.ShapeDtypeStruct((1, modes), F32),
        in_specs=[
            pl.BlockSpec(memory_space=pl.ANY),
            pl.BlockSpec(memory_space=pltpu.VMEM),
            pl.BlockSpec(memory_space=pltpu.VMEM),
        ],
        out_specs=pl.BlockSpec(memory_space=pltpu.VMEM),
        scratch_shapes=[
            pltpu.VMEM((2, padded, modes), BF16),
            pltpu.VMEM((2, padded, modes), BF16),
            pltpu.VMEM((2, rows, modes), BF16),
            pltpu.VMEM((2 * modes, padded), BF16),
            pltpu.VMEM((2 * modes, padded), BF16),
            pltpu.VMEM((tiles, 3, 2 * WIDE, WIDE), BF16),
            pltpu.VMEM((WIDE, WIDE), BF16),
            pltpu.VMEM((3 * SLOTS * PERIOD + 16 * SLOTS, PERIOD), BF16),
            pltpu.VMEM((TILE, TILE), BF16),
            pltpu.VMEM((tiles, PERIOD, WIDE), BF16),
            pltpu.VMEM((3 * SLOTS * PERIOD + 16 * SLOTS, WIDE), BF16),
            pltpu.VMEM((6 * modes, rows), BF16),
            pltpu.VMEM((6 * modes, rows), BF16),
            pltpu.VMEM((6 * modes, 2 * modes), F32),
            pltpu.VMEM((6 * modes, 2 * modes), F32),
            pltpu.VMEM((owners, 3 * PAIRS, modes // owners, modes), BF16),
            pltpu.VMEM((owners - 1, 3 * PAIRS, modes // owners, modes), BF16),
            pltpu.VMEM((6, 8, modes), F32),
            pltpu.VMEM((3 * owners, 8, modes), F32),
            dma((1,)),
            dma((2, tiles)),
            dma((2, 2, 2, tiles)),
            dma((2, 3)),
            dma((2, 2)),
            dma((2, 4)),
            dma((2, 3 * owners)),
        ],
        compiler_params=pltpu.CompilerParams(
            collective_id=0, has_side_effects=True, vmem_limit_bytes=56 * 1024 * 1024
        ),
        name="diffusivity",
    )(vectors, planes, frequency.reshape(blocks_all, modes))
    return result.reshape(modes)


def solution(mesh):
    return jax.shard_map(
        local,
        mesh=mesh,
        in_specs=(P("atom", "mode"), P(None, None, None, None, "atom"), P(None, "atom"), P()),
        out_specs=P("mode"),
        check_vma=False,
    )
```

profile of v0, /device:TPU:0, one launch (start us, length us, event | category | flops | bytes accessed | tf_op | source)
XLA Modules:
  0.0 61.7 jit_solution(1202872593309152200)
XLA Ops:
  0.0 0.0 copy-start
  0.0 0.1 pad.2.clone
  0.1 0.6 %copy-done = s32[4,1280]{1,0:T(4,128)S(1)} copy-done((s32[4,1280]{1,0:T(4,128)S(1)}, s32[4,1280]{1,0:T(4,128)}, u32[]{:S(2)}) %copy-start) | copy-done | bytes 20504
  0.8 1.1 %convert_bitcast_fusion = bf16[3,4,3,3,1280]{4,1,3,0,2:T(4,128)(2,1)S(1)} fusion(f32[4,3,3,3,1280]{4,0,3,2,1:T(4,128)} %param.5), kind=kLoop, calls=%fused_computation.1 | loop fusion | flops 138240 | bytes 829440 | tf_op jit(solution)/shard_map/convert_element_type | solution.py:558
  1.9 0.1 copy.6
  2.1 0.2 convert_element_type.14
  2.3 0.8 %maximum_maximum_fusion.planes_ref = bf16[3,48,1280]{2,1,0:T(8,128)(2,1)} fusion(bf16[3,4,1280]{2,1,0:T(4,128)(2,1)S(1)} %broadcast_in_dim.4, bf16[3,36,1280]{2,1,0:T(8,128)(2,1)S(1)} %convert_element_type.14, bf16[48]{0:T(256)(128)(2,1)S(1)} %pad.2.clone), kind=kLoop, calls=%fused_computation | loop fusion | flops 1105920 | bytes 675936 | tf_op jit(solution)/shard_map/concatenate | solution.py:559
  3.2 57.3 %diffusivity.1 = f32[1,128]{1,0:T(1,128)} custom-call(bf16[3840,128]{1,0:T(8,128)(2,1)} %vec.1, bf16[3,48,1280]{2,1,0:T(8,128)(2,1)} %maximum_maximum_fusion.planes_ref, f32[8,128]{1,0:T(8,128)} %bitcast.4), custom_call_target="tpu_custom_call" | custom-call | tf_op jit(solution)/shard_map/diffusivity/pallas_call | solution.py:569
  60.5 0.0 copy-start.1
  60.5 0.7 %copy-done.1 = f32[1,128]{1,0:T(1,128)S(1)} copy-done((f32[1,128]{1,0:T(1,128)S(1)}, f32[1,128]{1,0:T(1,128)}, u32[]{:S(2)}) %copy-start.1) | copy-done | bytes 536
  61.2 0.5 copy.8
  (4 shorter events, 0.0 us)
Async XLA Ops:
  0.0 0.7 %copy-start = (s32[4,1280]{1,0:T(4,128)S(1)}, s32[4,1280]{1,0:T(4,128)}, u32[]{:S(2)}) copy-start(s32[4,1280]{1,0:T(4,128)} %param.6) | copy-start | bytes 61444
  60.5 0.7 %copy-start.1 = (f32[1,128]{1,0:T(1,128)S(1)}, f32[1,128]{1,0:T(1,128)}, u32[]{:S(2)}) copy-start(f32[1,128]{1,0:T(1,128)} %diffusivity.1) | copy-start | bytes 1540
where the time goes:
time: 62 us; the launch traced here: 61.7 us
  Pallas kernels  57.3 us (92%)
  local copies, waits for them, and re-layouts  2.29 us (4%)
  other arithmetic  2.03 us (3%)
    pallas_call x1, Pallas kernels, local(): pl.pallas_call(functools.partial(kernel, sizes), out_shape=jax.ShapeDtype...  57.3 us
    unnamed x5, local copies, waits for them, and re-layouts  1.82 us

commit v1 on v0

v1 whole, which is shorter than its diff:
```python
import functools
import math

import jax
import jax.numpy as jnp
from jax import lax
from jax.experimental import pallas as pl
from jax.experimental.pallas import tpu as pltpu
from jax.sharding import PartitionSpec as P

HALO = 64
PARTNERS = 4
WIDTH_MODES = 320
TILE = 128
WIDE = 3 * TILE
EDGE = 3 * HALO
PERIOD = 48
SLOTS = 4
MESH = pl.DeviceIdType.MESH
BF16 = jnp.bfloat16
F32 = jnp.float32

SELF_PAIRS = ((0, 0), (1, 0), (1, 1))


def aligned(value):
    return pl.multiple_of(value, 16)


def band_groups(lane_tile):
    first = (TILE * lane_tile) // 3
    last = (TILE * lane_tile + TILE - 1) // 3
    down = range((3 * first) // PERIOD, (3 * (last + HALO - 2) + 2) // PERIOD + 1)
    up = range((3 * (HALO + first + 2)) // PERIOD, (3 * (2 * HALO + last) + 2) // PERIOD + 1)
    return down, up


def kernel(
    sizes,
    vec,
    couplings,
    neighbours,
    frequencies,
    out_ref,
    own,
    up,
    dn,
    own_t,
    up_t,
    raw,
    near,
    freq_ref,
    gathered,
    weights,
    spread,
    expand,
    eye,
    mixed,
    pattern,
    app_own,
    app_up,
    acc_next,
    acc_skip,
    acc_mixed,
    red_self,
    in_self,
    red_early,
    in_early,
    from_mate,
    red_next,
    in_next,
    red_skip,
    in_skip,
    in_mixed,
    given,
    taken,
    local_sem,
    y_sem,
    z_sem,
    edge_sem,
    side_sem,
    self_sem,
    early_sem,
    next_sem,
    skip_sem,
    mixed_sem,
    fin_sem,
):
    blocks_all, groups, rows_dev, modes, half_width = sizes
    rows = rows_dev // 2
    atoms = rows // 3
    tiles = rows // WIDE
    owners = 2 * groups
    share = modes // owners
    part = modes // groups

    mode = lax.axis_index("mode")
    atom = lax.axis_index("atom")
    s = mode // 2
    y = mode % 2
    other = 1 - y
    mate = mode + 1 - 2 * y
    h = (y + atom) % 2
    supers = blocks_all // 2
    has_up = s < supers - 1
    has_dn = s > 0
    outer = (atom + 2 * h - 1 + groups) % groups
    across = (atom + 1 - 2 * h + groups) % groups

    def remote(src, dst, sems, at, device):
        return pltpu.make_async_remote_copy(
            src_ref=src,
            dst_ref=dst,
            send_sem=sems.at[(0,) + at],
            recv_sem=sems.at[(1,) + at],
            device_id=device,
            device_id_type=MESH,
        )

    def local_copy():
        size = rows + EDGE
        return pltpu.make_async_copy(
            vec.at[pl.ds(aligned(h * (rows - EDGE)), size), :],
            own.at[y, pl.ds(aligned((1 - h) * EDGE), size), :],
            local_sem.at[0],
        )

    half_lanes = pl.ds(pl.multiple_of(h * atoms, TILE), atoms)
    loads = [
        pltpu.make_async_copy(couplings.at[:, :, half_lanes], raw, local_sem.at[1]),
        pltpu.make_async_copy(neighbours.at[:, half_lanes], near, local_sem.at[2]),
        pltpu.make_async_copy(frequencies, freq_ref, local_sem.at[3]),
    ]
    for load in loads:
        load.start()
    local_copy().start()

    barrier = pltpu.get_barrier_semaphore()

    def greet(device):
        pl.semaphore_signal(barrier, inc=1, device_id=device, device_id_type=MESH)

    pl.when(has_up)(lambda: greet((mode + 2, atom)))
    pl.when(has_dn)(lambda: greet((mode - 2, atom)))
    for step in range(groups):
        slab = (atom + step) % groups
        greet((mate, slab))
        if step:
            greet((mode, slab))
    sides = has_up.astype(jnp.int32) + has_dn.astype(jnp.int32)
    pl.semaphore_wait(barrier, owners - 1 + sides)

    def y_copy(t):
        return remote(
            vec.at[pl.ds(aligned((1 - h) * rows + t * WIDE), WIDE), :],
            own.at[y, pl.ds(aligned(EDGE + t * WIDE), WIDE), :],
            y_sem,
            (t,),
            (mate, atom),
        )

    def y_edge():
        return remote(
            vec.at[pl.ds(aligned(rows - EDGE + h * EDGE), EDGE), :],
            own.at[y, pl.ds(aligned(h * (rows + EDGE)), EDGE), :],
            edge_sem,
            (0,),
            (mate, atom),
        )

    def outer_edge():
        return remote(
            vec.at[pl.ds(aligned(h * (rows_dev - EDGE)), EDGE), :],
            own.at[y, pl.ds(aligned((1 - h) * (rows + EDGE)), EDGE), :],
            edge_sem,
            (1,),
            (mode, outer),
        )

    def across_edge():
        return remote(
            vec.at[pl.ds(aligned((1 - h) * (rows_dev - EDGE)), EDGE), :],
            own.at[y, pl.ds(aligned(h * (rows + EDGE)), EDGE), :],
            edge_sem,
            (2,),
            (mate, across),
        )

    def z_copy(upward, relay, t):
        if relay:
            src = own.at[other, pl.ds(aligned(EDGE + t * WIDE), WIDE), :]
        else:
            src = vec.at[pl.ds(aligned(h * rows + t * WIDE), WIDE), :]
        if upward:
            dst = dn.at[relay, pl.ds(aligned(t * WIDE), WIDE), :]
            return remote(src, dst, z_sem, (0, relay, t), (mode + 2, atom))
        dst = up.at[relay, pl.ds(aligned(EDGE + t * WIDE), WIDE), :]
        return remote(src, dst, z_sem, (1, relay, t), (mode - 2, atom))

    def side_copy(relay, inner):
        if inner:
            src = EDGE + (1 - h) * (rows - EDGE)
            dst = h * (rows + EDGE)
            device = (mate, atom)
            place = 1 - relay
        else:
            src = EDGE + h * (rows - EDGE)
            dst = (1 - h) * (rows + EDGE)
            device = (mode, outer)
            place = relay
        return pltpu.make_async_remote_copy(
            src_ref=up.at[relay, pl.ds(aligned(src), EDGE), :],
            dst_ref=up.at[place, pl.ds(aligned(dst), EDGE), :],
            send_sem=side_sem.at[0, relay, inner],
            recv_sem=side_sem.at[1, place, inner],
            device_id=device,
            device_id_type=MESH,
        )

    def side_wait(place, inner):
        return pltpu.make_async_remote_copy(
            src_ref=up.at[place, pl.ds(0, EDGE), :],
            dst_ref=up.at[place, pl.ds(0, EDGE), :],
            send_sem=side_sem.at[0, place, inner],
            recv_sem=side_sem.at[1, place, inner],
            device_id=(mate, atom),
            device_id_type=MESH,
        )

    order = [tiles - 1] + list(range(tiles - 1))
    for at, t in enumerate(order):
        y_copy(t).start()

        @pl.when(has_up)
        def _():
            z_copy(1, 0, t).start()

        @pl.when(has_dn)
        def _():
            z_copy(0, 0, t).start()

        if at == 1:
            y_edge().start()
            outer_edge().start()
            across_edge().start()

    @pl.when(jnp.logical_not(has_dn))
    def _():
        taken[0:owners] = jnp.zeros((owners, 8, modes), F32)

    @pl.when(jnp.logical_not(has_up))
    def _():
        taken[2 * owners : 3 * owners] = jnp.zeros((owners, 8, modes), F32)

    given[...] = jnp.zeros((6, 8, modes), F32)

    row = lax.broadcasted_iota(jnp.int32, (WIDE, WIDE), 0)
    col = lax.broadcasted_iota(jnp.int32, (WIDE, WIDE), 1)
    spread[...] = jnp.where(col == 3 * (row % TILE) + row // TILE, 1.0, 0.0).astype(BF16)
    row = lax.broadcasted_iota(jnp.int32, (TILE, TILE), 0)
    col = lax.broadcasted_iota(jnp.int32, (TILE, TILE), 1)
    eye[...] = jnp.where(row == col, 1.0, 0.0).astype(BF16)
    height = 3 * SLOTS * PERIOD
    row = lax.broadcasted_iota(jnp.int32, (height + 16 * SLOTS, PERIOD), 0)
    col = lax.broadcasted_iota(jnp.int32, (height + 16 * SLOTS, PERIOD), 1)
    pair = row // PERIOD
    value_col = (3 * (pair % 3) + (row % PERIOD) % 3) * SLOTS + pair // 3
    place_col = 9 * SLOTS + (row - height) // 16
    want = jnp.where(row < height, value_col, place_col)
    expand[...] = jnp.where(col == want, 1.0, 0.0).astype(BF16)

    for load in loads:
        load.wait()
    lane = lax.broadcasted_iota(jnp.int32, (SLOTS, atoms), 1)
    here = atom * (2 * atoms) + h * atoms + lane
    offset = near[...] - here
    total_atoms = 2 * atoms * groups
    offset = jnp.where(offset > HALO, offset - total_atoms, offset)
    offset = jnp.where(offset < -HALO, offset + total_atoms, offset)
    place = (offset + HALO + lane % TILE).astype(F32)
    for p in range(3):
        for a in range(3):
            for q in range(3):
                first = SLOTS * (3 * a + q)
                gathered[p, first : first + SLOTS, :] = raw[9 * a + 3 * p + q]
        gathered[p, 9 * SLOTS : 10 * SLOTS, :] = place
        gathered[p, 10 * SLOTS : PERIOD, :] = jnp.zeros((PERIOD - 10 * SLOTS, atoms), F32)
    stacked = []
    for t in range(tiles):
        lanes = slice(t * TILE, (t + 1) * TILE)
        stacked.append(
            jnp.concatenate([gathered[p, :, lanes].astype(BF16) for p in range(3)], axis=1)
        )
    stacked = jnp.concatenate(stacked, axis=0)
    mixed[...] = (
        jnp.dot(stacked, spread[...], preferred_element_type=F32)
        .astype(BF16)
        .reshape(tiles, PERIOD, WIDE)
    )

    atom_row = (lax.broadcasted_iota(jnp.int32, (PERIOD, TILE), 0) // 3).astype(F32).astype(BF16)
    atom_row = atom_row.reshape(3, 16, TILE)

    def build(t):
        pattern[...] = jnp.dot(expand[...], mixed[t], preferred_element_type=F32).astype(BF16)
        for lane_tile in range(3):
            lanes = slice(lane_tile * TILE, (lane_tile + 1) * TILE)
            down, above = band_groups(lane_tile)
            for g in range(2 * WIDE // PERIOD):
                slots = ([0, 1] if g in above else []) + ([2, 3] if g in down else [])
                span = slice(g * PERIOD, (g + 1) * PERIOD)
                if not slots:
                    for a in range(3):
                        weights[t, a, span, lanes] = jnp.zeros((PERIOD, TILE), BF16)
                    continue
                here = atom_row + jnp.asarray(16.0 * g, BF16)
                flags = {}
                for k in slots:
                    target = pattern[height + 16 * k : height + 16 * (k + 1), lanes]
                    flags[k] = here == target[None]
                for a in range(3):
                    total = None
                    for k in slots:
                        first = (3 * k + a) * PERIOD
                        value = pattern[first : first + PERIOD, lanes].reshape(3, 16, TILE)
                        term = jnp.where(flags[k], value, jnp.zeros_like(value))
                        total = term if total is None else total + term
                    weights[t, a, span, lanes] = total.reshape(PERIOD, TILE)

    def build_step(t, carry):
        build(t)
        return carry

    lax.fori_loop(0, tiles, build_step, 0)

    def transposed(source, target, u):
        span = pl.ds(pl.multiple_of(u * WIDE, WIDE), WIDE)
        target[:, span] = lax.dot_general(
            eye[...], source[span, :], (((1,), (1,)), ((), ())), preferred_element_type=F32
        ).astype(BF16)

    def apply_own(t):
        window = own_t[:, t * WIDE : (t + 2) * WIDE]
        for a in range(3):
            app_own[a * 2 * modes : (a + 1) * 2 * modes, t * WIDE : (t + 1) * WIDE] = jnp.dot(
                window, weights[t, a], preferred_element_type=F32
            ).astype(BF16)

    def apply_up(relay, t):
        window = up_t[relay, :, t * WIDE : (t + 2) * WIDE]
        for a in range(3):
            app_up[relay, a * modes : (a + 1) * modes, t * WIDE : (t + 1) * WIDE] = jnp.dot(
                window, weights[t, a], preferred_element_type=F32
            ).astype(BF16)

    def schedule(arrived, edges, moved, done):
        blocks = []
        for u in range(tiles + 1):
            need = {v for v in (u - 1, u) if 0 <= v < tiles}
            if u not in moved and need <= arrived and (edges or 0 < u < tiles):
                blocks.append(u)
                moved.add(u)
        ready = [v for v in range(tiles) if v not in done and {v, v + 1} <= moved]
        done.update(ready)
        return blocks, ready

    def own_step(arrived, edges, moved, done):
        blocks, ready = schedule(arrived, edges, moved, done)
        for u in blocks:
            for j in range(2):
                transposed(own.at[j], own_t.at[j * modes : (j + 1) * modes], u)
        for v in ready:
            apply_own(v)

    local_copy().wait()
    moved, done, arrived = set(), set(), set()
    for at, t in enumerate(order):
        y_copy(t).wait_recv()

        @pl.when(has_up)
        def _():
            z_copy(1, 1, t).start()

        @pl.when(has_dn)
        def _():
            z_copy(0, 1, t).start()

        arrived.add(t)
        if at == 3:
            y_edge().wait_recv()
            outer_edge().wait_recv()
            across_edge().wait_recv()
        if at == 2:

            @pl.when(has_up)
            def _():
                for v in order[:2]:
                    z_copy(0, 0, v).wait_recv()
                side_copy(0, 0).start()
                side_copy(0, 1).start()

        own_step(arrived, at >= 3, moved, done)

    bits = []
    bit = 1
    while bit < groups:
        side = (atom // bit) % 2
        bits.append((side, (mode, atom + bit * (1 - 2 * side))))
        bit *= 2
    mate_bit = (y, (mate, atom))

    class Halving:
        def __init__(self, buffer, landing, sems, stages):
            self.buffer, self.landing, self.sems, self.stages = buffer, landing, sems, stages
            self.base, self.size, self.at, self.stage = 0, buffer.shape[0], 0, 0
            self.copies = []

        def send(self):
            side, device = self.stages[self.stage]
            self.size //= 2
            self.keep = self.base + side * self.size
            copy = remote(
                self.buffer.at[pl.ds(self.base + (1 - side) * self.size, self.size)],
                self.landing.at[pl.ds(self.at, self.size)],
                self.sems,
                (self.stage,),
                device,
            )
            copy.start()
            self.copies.append(copy)

        def receive(self):
            self.copies[-1].wait_recv()
            for i in range(self.size):
                self.buffer[self.keep + i] = (
                    self.buffer[self.keep + i].astype(F32)
                    + self.landing[self.at + i].astype(F32)
                ).astype(BF16)
            self.at += self.size
            self.base = self.keep
            self.stage += 1

    def store(buffer, index, piece):
        count = buffer.shape[0]
        buffer[:, index] = piece.astype(BF16).reshape(count, modes // count, modes)

    own_main = jnp.concatenate([own[j, EDGE : EDGE + rows, :] for j in range(2)], axis=1)
    for a in range(3):
        product = jnp.dot(
            app_own[a * 2 * modes : (a + 1) * 2 * modes, :],
            own_main,
            preferred_element_type=F32,
        )
        for at, (c, b) in enumerate(SELF_PAIRS):
            store(
                red_self,
                3 * at + a,
                product[c * modes : (c + 1) * modes, b * modes : (b + 1) * modes],
            )
    self_sum = Halving(red_self, in_self, self_sem, bits + [mate_bit])
    self_sum.send()

    def await_chunks(relay, from_up, from_dn):
        @pl.when(has_up)
        def _():
            for t in from_up:
                z_copy(0, relay, t).wait_recv()

        @pl.when(has_dn)
        def _():
            for t in from_dn:
                z_copy(1, relay, t).wait_recv()

    await_chunks(0, order[2:], order)
    for a in range(3):
        product = jnp.dot(
            app_own[a * 2 * modes : (a + 1) * 2 * modes, :],
            up[0, EDGE : EDGE + rows, :],
            preferred_element_type=F32,
        )
        for c in range(2):
            store(red_early, 3 * c + a, product[c * modes : (c + 1) * modes])
    self_sum.receive()
    self_sum.send()

    @pl.when(has_up)
    def _():
        side_wait(0, 0).wait_recv()

    for u in range(1, tiles):
        transposed(up.at[0], up_t.at[0], u)
    for v in range(1, tiles - 1):
        apply_up(0, v)

    def add_next(t, start):
        for a in range(3):
            rows_a = slice(a * 2 * modes, (a + 1) * 2 * modes)
            term = jnp.dot(
                app_own[rows_a, t * WIDE : (t + 1) * WIDE],
                up[1, EDGE + t * WIDE : EDGE + (t + 1) * WIDE, :],
                preferred_element_type=F32,
            )
            acc_next[rows_a, :] = term if start else acc_next[rows_a, :] + term

    def add_skip(t, start):
        span = slice(t * WIDE, (t + 1) * WIDE)
        term = jnp.dot(app_up[1, :, span], dn[1, span, :], preferred_element_type=F32)
        acc_skip[...] = term if start else acc_skip[...] + term
        term = jnp.dot(app_up[y, :, span], dn[other, span, :], preferred_element_type=F32)
        acc_mixed[...] = term if start else acc_mixed[...] + term

    early_sum = Halving(red_early, in_early, early_sem, bits)

    def hand_over():
        return remote(red_early.at[early_sum.base], from_mate, early_sem, (len(bits),), mate_bit[1])

    def finish_direct():
        @pl.when(has_up)
        def _():
            side_wait(0, 1).wait_recv()

        for u in (0, tiles):
            transposed(up.at[0], up_t.at[0], u)
        for v in (0, tiles - 1):
            apply_up(0, v)
        product = jnp.dot(app_up[0], dn[0], preferred_element_type=F32)
        for a in range(3):
            store(red_early, 6 + a, product[a * modes : (a + 1) * modes])

    moved, done, arrived = set(), set(), set()
    started = False
    for at, t in enumerate(order):
        await_chunks(1, [t], [t])
        arrived.add(t)
        if at == 1:

            @pl.when(has_up)
            def _():
                side_copy(1, 0).start()
                side_copy(1, 1).start()

        add_next(t, at == 0)
        if at == 1:
            self_sum.receive()
            self_sum.send()
        if at == 2:
            finish_direct()
            early_sum.send()

            @pl.when(has_up)
            def _():
                side_wait(1, 0).wait_recv()
                side_wait(1, 1).wait_recv()

        if at == 3:
            self_sum.receive()
            early_sum.receive()
            early_sum.send()
        if at == tiles - 1:
            early_sum.receive()
            handed = hand_over()
            handed.start()
            for a in range(3):
                for c in range(2):
                    first = a * 2 * modes + c * modes
                    store(red_next, 3 * c + a, acc_next[first : first + modes, :])
            next_sum = Halving(red_next, in_next, next_sem, bits)
            next_sum.send()
        if at >= 2:
            blocks, ready = schedule(arrived, True, moved, done)
            for u in blocks:
                transposed(up.at[1], up_t.at[1], u)
            for v in ready:
                apply_up(1, v)
                add_skip(v, not started)
                started = True

    for a in range(3):
        rows_a = slice(a * modes, (a + 1) * modes)
        store(red_skip, a, acc_skip[rows_a, :])
        store(red_skip, 3 + a, acc_mixed[rows_a, :])
    skip_sum = Halving(red_skip, in_skip, skip_sem, bits[:-1])
    for _ in bits[:-1]:
        skip_sum.send()
        next_sum.receive()
        next_sum.send()
        skip_sum.receive()
    side, last = bits[-1]
    keep = skip_sum.base + side
    pass_on = skip_sum.base + 1 - side
    mine_rows = pl.ds(aligned(y * share), share)
    mate_rows = pl.ds(aligned(other * share), share)
    last_copies = [
        remote(
            red_skip.at[pass_on, pl.ds(0, 3)],
            in_skip.at[in_skip.shape[0] - 1, pl.ds(0, 3)],
            mixed_sem,
            (0,),
            last,
        ),
        remote(
            red_skip.at[pass_on, pl.ds(3, 3), mine_rows], in_mixed.at[0], mixed_sem, (1,), last
        ),
        remote(
            red_skip.at[keep, pl.ds(3, 3), mate_rows], in_mixed.at[1], mixed_sem, (2,), mate_bit[1]
        ),
        remote(
            red_skip.at[pass_on, pl.ds(3, 3), mate_rows],
            in_mixed.at[2],
            mixed_sem,
            (3,),
            (mate, last[1]),
        ),
    ]
    for copy in last_copies:
        copy.start()

    def frequency(block):
        index = jnp.clip(block, 0, blocks_all - 1)
        return freq_ref[pl.ds(index, 1), :]

    def account(values, first_row, count, c_index, b_index, valid, same=False):
        lane = lax.broadcasted_iota(jnp.int32, (count, modes), 1)
        spot = lane == lax.broadcasted_iota(jnp.int32, (count, modes), 0) + first_row
        squares = None
        for value in values:
            square = value * value
            squares = square if squares is None else squares + square
        c_row = frequency(2 * s - 2 + c_index)
        b_row = frequency(2 * s - 2 + b_index)
        c_col = jnp.sum(jnp.where(spot, c_row, 0.0), axis=1, keepdims=True)
        offset = b_row - c_col
        terms = squares * (half_width / math.pi / (offset * offset + half_width * half_width))
        if valid is not None:
            terms = jnp.where(valid, terms, 0.0)

        def folded(value):
            return jnp.sum(value.reshape(count // 8, 8, modes), axis=0)

        given[b_index] = given[b_index] + folded(terms)
        if not same:
            col_sum = jnp.sum(terms, axis=1, keepdims=True)
            given[c_index] = given[c_index] + folded(jnp.where(spot, col_sum, 0.0))

    for at, (c, b) in enumerate(SELF_PAIRS):
        values = [red_self[self_sum.base, 3 * at + a].astype(F32) for a in range(3)]
        account(values, self_sum.base * share, share, 2 + c, 2 + b, None, c == b)

    handed.wait_recv()
    next_sum.receive()
    spot_row = next_sum.base * part
    for c in range(2):
        values = [
            red_next[next_sum.base, 3 * c + a].astype(F32) + from_mate[3 * c + a].astype(F32)
            for a in range(3)
        ]
        account(values, spot_row, part, 2 + c, 4 + other, has_up)

    both = jnp.logical_and(has_up, has_dn)
    for copy in last_copies:
        copy.wait_recv()
    values = [
        red_skip[keep, a].astype(F32)
        + in_skip[in_skip.shape[0] - 1, a].astype(F32)
        + from_mate[6 + a].astype(F32)
        for a in range(3)
    ]
    account(values, keep * part, part, 4 + other, other, both)
    values = []
    for a in range(3):
        value = red_skip[keep, 3 + a, mine_rows].astype(F32)
        for i in range(3):
            value = value + in_mixed[i, a].astype(F32)
        values.append(value)
    account(values, keep * part + y * share, share, 4, 1, both)

    rank = y * groups + atom

    def final_copy(delta, side, slab):
        slot = (1 - delta) * owners + rank
        return pltpu.make_async_remote_copy(
            src_ref=given.at[2 * (delta + 1) + side],
            dst_ref=taken.at[slot],
            send_sem=fin_sem.at[0, (delta + 1) * owners + side * groups + slab],
            recv_sem=fin_sem.at[1, slot],
            device_id=(2 * (s + delta) + side, slab),
            device_id_type=MESH,
        )

    def final_wait(delta, side, slab):
        slot = (delta + 1) * owners + side * groups + slab
        return pltpu.make_async_remote_copy(
            src_ref=given.at[0],
            dst_ref=taken.at[slot],
            send_sem=fin_sem.at[0, slot],
            recv_sem=fin_sem.at[1, slot],
            device_id=(2 * (s + delta) + side, slab),
            device_id_type=MESH,
        )

    def for_all(action):
        for delta, valid in ((0, None), (1, has_up), (-1, has_dn)):
            for side in range(2):
                for slab in range(groups):
                    if valid is None:
                        condition = jnp.logical_or(side != y, slab != atom)
                    else:
                        condition = valid
                    pl.when(condition)(functools.partial(action, delta, side, slab))

    for_all(lambda *at: final_copy(*at).start())
    taken[owners + rank] = given[2 + y]
    for_all(lambda *at: final_wait(*at).wait_recv())
    total = jnp.sum(jnp.sum(taken[...], axis=0), axis=0, keepdims=True)
    own_freq = frequency(mode)
    out_ref[...] = total / (own_freq * own_freq)

    for_all(lambda *at: final_copy(*at).wait_send())
    for copy in self_sum.copies + early_sum.copies + next_sum.copies + skip_sum.copies:
        copy.wait_send()
    for copy in last_copies + [handed]:
        copy.wait_send()
    y_edge().wait_send()
    outer_edge().wait_send()
    across_edge().wait_send()
    for t in range(tiles):
        y_copy(t).wait_send()

    @pl.when(has_up)
    def _():
        for relay in range(2):
            side_copy(relay, 0).wait_send()
            side_copy(relay, 1).wait_send()
            for t in range(tiles):
                z_copy(1, relay, t).wait_send()

    @pl.when(has_dn)
    def _():
        for relay in range(2):
            for t in range(tiles):
                z_copy(0, relay, t).wait_send()


def local(vectors, couplings, neighbours, frequency):
    rows_dev, modes = vectors.shape
    blocks_all = lax.axis_size("mode")
    groups = lax.axis_size("atom")
    half_width = WIDTH_MODES / (modes * blocks_all)
    rows = rows_dev // 2
    tiles = rows // WIDE
    padded = rows + 2 * EDGE
    owners = 2 * groups
    share = modes // owners
    part = modes // groups
    levels = groups.bit_length() - 1

    blocks = couplings.transpose(1, 2, 3, 0, 4).reshape(27, SLOTS, rows_dev // 3)
    sizes = (blocks_all, groups, rows_dev, modes, half_width)
    dma = pltpu.SemaphoreType.DMA
    result = pl.pallas_call(
        functools.partial(kernel, sizes),
        out_shape=jax.ShapeDtypeStruct((1, modes), F32),
        in_specs=[pl.BlockSpec(memory_space=pltpu.HBM)] * 4,
        out_specs=pl.BlockSpec(memory_space=pltpu.VMEM),
        scratch_shapes=[
            pltpu.VMEM((2, padded, modes), BF16),
            pltpu.VMEM((2, padded, modes), BF16),
            pltpu.VMEM((2, rows, modes), BF16),
            pltpu.VMEM((2 * modes, padded), BF16),
            pltpu.VMEM((2, modes, padded), BF16),
            pltpu.VMEM((27, SLOTS, rows // 3), F32),
            pltpu.VMEM((SLOTS, rows // 3), jnp.int32),
            pltpu.VMEM((blocks_all, modes), F32),
            pltpu.VMEM((3, PERIOD, rows // 3), F32),
            pltpu.VMEM((tiles, 3, 2 * WIDE, WIDE), BF16),
            pltpu.VMEM((WIDE, WIDE), BF16),
            pltpu.VMEM((3 * SLOTS * PERIOD + 16 * SLOTS, PERIOD), BF16),
            pltpu.VMEM((TILE, TILE), BF16),
            pltpu.VMEM((tiles, PERIOD, WIDE), BF16),
            pltpu.VMEM((3 * SLOTS * PERIOD + 16 * SLOTS, WIDE), BF16),
            pltpu.VMEM((6 * modes, rows), BF16),
            pltpu.VMEM((2, 3 * modes, rows), BF16),
            pltpu.VMEM((6 * modes, modes), F32),
            pltpu.VMEM((3 * modes, modes), F32),
            pltpu.VMEM((3 * modes, modes), F32),
            pltpu.VMEM((owners, 9, share, modes), BF16),
            pltpu.VMEM((owners - 1, 9, share, modes), BF16),
            pltpu.VMEM((groups, 9, part, modes), BF16),
            pltpu.VMEM((groups - 1, 9, part, modes), BF16),
            pltpu.VMEM((9, part, modes), BF16),
            pltpu.VMEM((groups, 6, part, modes), BF16),
            pltpu.VMEM((groups - 1, 6, part, modes), BF16),
            pltpu.VMEM((groups, 6, part, modes), BF16),
            pltpu.VMEM((groups - 1, 6, part, modes), BF16),
            pltpu.VMEM((3, 3, share, modes), BF16),
            pltpu.VMEM((6, 8, modes), F32),
            pltpu.VMEM((3 * owners, 8, modes), F32),
            dma((4,)),
            dma((2, tiles)),
            dma((2, 2, 2, tiles)),
            dma((2, 3)),
            dma((2, 2, 2)),
            dma((2, levels + 1)),
            dma((2, levels + 1)),
            dma((2, levels)),
            dma((2, levels)),
            dma((2, 4)),
            dma((2, 3 * owners)),
        ],
        compiler_params=pltpu.CompilerParams(
            collective_id=0, has_side_effects=True, vmem_limit_bytes=56 * 1024 * 1024
        ),
        name="diffusivity",
    )(vectors, blocks, neighbours, frequency.reshape(blocks_all, modes))
    return result.reshape(modes) * (math.pi / 3.0)


def solution(mesh):
    return jax.shard_map(
        local,
        mesh=mesh,
        in_specs=(P("atom", "mode"), P(None, None, None, None, "atom"), P(None, "atom"), P()),
        out_specs=P("mode"),
        check_vma=False,
    )
```

time: 62 us -> 48.6 us (0.78)
  Pallas kernels: 57.3 us -> 47.3 us
  local copies, waits for them, and re-layouts: 2.29 us -> 0 us
  other arithmetic: 2.03 us -> 1.19 us
    pallas_call x1, Pallas kernels: 57.3 us -> 47.3 us  [local(): pl.pallas_call(functools.partial(kernel, sizes), out_shape=jax.ShapeDtype...]
    unnamed x5 -> x0, local copies, waits for them, and re-layouts: 1.82 us -> none
    mul x0 -> x1, other arithmetic: none -> 1.19 us  [local(): return result.reshape(modes) * (math.pi / 3.0)]
    convert_element_type x2 -> x0, other arithmetic: 1.17 us -> none  [the longest x1 1.15 us: local(): couplings.transpose(2, 0, 1, 3, 4).reshape(3, 9 * SLOTS, atoms_dev)]
    concatenate x1 -> x0, other arithmetic: 0.85 us -> none  [local(): jnp.concatenate([values, jnp.broadcast_to(window[None], (3, SLOTS, atoms_...]
where the time goes in v1:
time: 48.6 us; the launch traced here: 48.5 us
  Pallas kernels  47.3 us (97%)
  other arithmetic  1.19 us (2%)
    pallas_call x1, Pallas kernels, local(): pl.pallas_call(functools.partial(kernel, sizes), out_shape=jax.ShapeDtype...  47.3 us
    mul x1, other arithmetic, local(): return result.reshape(modes) * (math.pi / 3.0)  1.19 us

profile of v1, /device:TPU:0, one launch (start us, length us, event | category | flops | bytes accessed | tf_op | source)
XLA Modules:
  0.0 48.5 jit_solution(13013511423854184692)
XLA Ops:
  0.0 47.3 %diffusivity.1 = f32[1,128]{1,0:T(1,128)} custom-call(bf16[3840,128]{1,0:T(8,128)(2,1)} %vec.1, f32[27,4,1280]{2,1,0:T(4,128)} %bitcast.6, s32[4,1280]{1,0:T(4,128)} %neighbours.1, f32[8,128]{1,0:T(8,128)} %bitcast.7), custom_call_target="tpu_custom_call" | custom-call | tf_op jit(solution)/shard_map/diffusivity/pallas_call | solution.py:760
  47.3 1.2 %multiply_bitcast_fusion = f32[128]{0:T(128)} fusion(f32[1,128]{1,0:T(1,128)} %diffusivity.1), kind=kLoop, calls=%fused_computation | loop fusion | flops 128 | bytes 1024 | tf_op jit(solution)/shard_map/mul | solution.py:815

commit v2 on v1

--- a/solution.py
+++ b/solution.py
@@ -66,6 +66,8 @@
     in_self,
     red_early,
     in_early,
+    red_direct,
+    in_direct,
     from_mate,
     red_next,
     in_next,
@@ -73,6 +75,7 @@
     in_skip,
     in_mixed,
     given,
+    packed,
     taken,
     local_sem,
     y_sem,
@@ -81,6 +84,7 @@
     side_sem,
     self_sem,
     early_sem,
+    direct_sem,
     next_sem,
     skip_sem,
     mixed_sem,
@@ -339,10 +343,10 @@
             eye[...], source[span, :], (((1,), (1,)), ((), ())), preferred_element_type=F32
         ).astype(BF16)
 
-    def apply_own(t):
-        window = own_t[:, t * WIDE : (t + 2) * WIDE]
+    def apply_own(parity, t):
+        window = own_t[parity, :, t * WIDE : (t + 2) * WIDE]
         for a in range(3):
-            app_own[a * 2 * modes : (a + 1) * 2 * modes, t * WIDE : (t + 1) * WIDE] = jnp.dot(
+            app_own[parity, a * modes : (a + 1) * modes, t * WIDE : (t + 1) * WIDE] = jnp.dot(
                 window, weights[t, a], preferred_element_type=F32
             ).astype(BF16)
 
@@ -353,28 +357,18 @@
                 window, weights[t, a], preferred_element_type=F32
             ).astype(BF16)
 
-    def schedule(arrived, edges, moved, done):
+    def schedule(arrived, moved, done):
         blocks = []
         for u in range(tiles + 1):
             need = {v for v in (u - 1, u) if 0 <= v < tiles}
-            if u not in moved and need <= arrived and (edges or 0 < u < tiles):
+            if u not in moved and need <= arrived:
                 blocks.append(u)
                 moved.add(u)
         ready = [v for v in range(tiles) if v not in done and {v, v + 1} <= moved]
         done.update(ready)
         return blocks, ready
 
-    def own_step(arrived, edges, moved, done):
-        blocks, ready = schedule(arrived, edges, moved, done)
-        for u in blocks:
-            for j in range(2):
-                transposed(own.at[j], own_t.at[j * modes : (j + 1) * modes], u)
-        for v in ready:
-            apply_own(v)
-
-    local_copy().wait()
-    moved, done, arrived = set(), set(), set()
-    for at, t in enumerate(order):
+    def forward(t):
         y_copy(t).wait_recv()
 
         @pl.when(has_up)
@@ -385,21 +379,54 @@
         def _():
             z_copy(0, 1, t).start()
 
-        arrived.add(t)
-        if at == 3:
-            y_edge().wait_recv()
-            outer_edge().wait_recv()
-            across_edge().wait_recv()
-        if at == 2:
-
-            @pl.when(has_up)
-            def _():
-                for v in order[:2]:
-                    z_copy(0, 0, v).wait_recv()
-                side_copy(0, 0).start()
-                side_copy(0, 1).start()
-
-        own_step(arrived, at >= 3, moved, done)
+    def await_chunks(relay, from_up, from_dn):
+        @pl.when(has_up)
+        def _():
+            for t in from_up:
+                z_copy(0, relay, t).wait_recv()
+
+        @pl.when(has_dn)
+        def _():
+            for t in from_dn:
+                z_copy(1, relay, t).wait_recv()
+
+    forward(order[0])
+    local_copy().wait()
+    outer_edge().wait_recv()
+    for u in range(tiles + 1):
+        transposed(own.at[y], own_t.at[y], u)
+    for v in range(tiles):
+        apply_own(y, v)
+        if v == 1:
+            forward(order[1])
+    await_chunks(0, order[:2], [])
+
+    @pl.when(has_up)
+    def _():
+        side_copy(0, 0).start()
+        side_copy(0, 1).start()
+
+    await_chunks(0, order[2:3], [])
+    transposed(up.at[0], up_t.at[0], 1)
+    forward(order[2])
+    await_chunks(0, order[3:4], [])
+    transposed(up.at[0], up_t.at[0], 2)
+    apply_up(0, 1)
+    forward(order[3])
+    await_chunks(0, order[4:], order)
+    for u in range(3, tiles):
+        transposed(up.at[0], up_t.at[0], u)
+    for v in range(2, tiles - 1):
+        apply_up(0, v)
+    forward(order[4])
+    for t in order[5:]:
+        forward(t)
+    y_edge().wait_recv()
+    across_edge().wait_recv()
+    for u in range(tiles + 1):
+        transposed(own.at[other], own_t.at[other], u)
+    for v in range(tiles):
+        apply_own(other, v)
 
     bits = []
     bit = 1
@@ -444,63 +471,32 @@
         count = buffer.shape[0]
         buffer[:, index] = piece.astype(BF16).reshape(count, modes // count, modes)
 
-    own_main = jnp.concatenate([own[j, EDGE : EDGE + rows, :] for j in range(2)], axis=1)
-    for a in range(3):
-        product = jnp.dot(
-            app_own[a * 2 * modes : (a + 1) * 2 * modes, :],
-            own_main,
-            preferred_element_type=F32,
-        )
-        for at, (c, b) in enumerate(SELF_PAIRS):
-            store(
-                red_self,
-                3 * at + a,
-                product[c * modes : (c + 1) * modes, b * modes : (b + 1) * modes],
-            )
+    early_sum = Halving(red_early, in_early, early_sem, bits)
+    for c in range(2):
+        product = jnp.dot(app_own[c], up[0, EDGE : EDGE + rows, :], preferred_element_type=F32)
+        for a in range(3):
+            store(red_early, 3 * c + a, product[a * modes : (a + 1) * modes])
+    early_sum.send()
+    for at, (c, b) in enumerate(SELF_PAIRS):
+        product = jnp.dot(app_own[c], own[b, EDGE : EDGE + rows, :], preferred_element_type=F32)
+        for a in range(3):
+            store(red_self, 3 * at + a, product[a * modes : (a + 1) * modes])
     self_sum = Halving(red_self, in_self, self_sem, bits + [mate_bit])
-    self_sum.send()
-
-    def await_chunks(relay, from_up, from_dn):
-        @pl.when(has_up)
-        def _():
-            for t in from_up:
-                z_copy(0, relay, t).wait_recv()
-
-        @pl.when(has_dn)
-        def _():
-            for t in from_dn:
-                z_copy(1, relay, t).wait_recv()
-
-    await_chunks(0, order[2:], order)
-    for a in range(3):
-        product = jnp.dot(
-            app_own[a * 2 * modes : (a + 1) * 2 * modes, :],
-            up[0, EDGE : EDGE + rows, :],
-            preferred_element_type=F32,
-        )
-        for c in range(2):
-            store(red_early, 3 * c + a, product[c * modes : (c + 1) * modes])
-    self_sum.receive()
     self_sum.send()
 
     @pl.when(has_up)
     def _():
         side_wait(0, 0).wait_recv()
 
-    for u in range(1, tiles):
-        transposed(up.at[0], up_t.at[0], u)
-    for v in range(1, tiles - 1):
-        apply_up(0, v)
-
     def add_next(t, start):
-        for a in range(3):
-            rows_a = slice(a * 2 * modes, (a + 1) * 2 * modes)
+        span = slice(t * WIDE, (t + 1) * WIDE)
+        for c in range(2):
             term = jnp.dot(
-                app_own[rows_a, t * WIDE : (t + 1) * WIDE],
+                app_own[c, :, span],
                 up[1, EDGE + t * WIDE : EDGE + (t + 1) * WIDE, :],
                 preferred_element_type=F32,
             )
-            acc_next[rows_a, :] = term if start else acc_next[rows_a, :] + term
+            acc_next[c] = term if start else acc_next[c] + term
 
     def add_skip(t, start):
         span = slice(t * WIDE, (t + 1) * WIDE)
@@ -509,10 +505,18 @@
         term = jnp.dot(app_up[y, :, span], dn[other, span, :], preferred_element_type=F32)
         acc_mixed[...] = term if start else acc_mixed[...] + term
 
-    early_sum = Halving(red_early, in_early, early_sem, bits)
-
-    def hand_over():
-        return remote(red_early.at[early_sum.base], from_mate, early_sem, (len(bits),), mate_bit[1])
+    direct_sum = Halving(red_direct, in_direct, direct_sem, bits)
+
+    def hand_over(source, place, sems):
+        copy = remote(
+            source.buffer.at[source.base],
+            from_mate.at[pl.ds(place, source.buffer.shape[1])],
+            sems,
+            (len(bits),),
+            mate_bit[1],
+        )
+        copy.start()
+        return copy
 
     def finish_direct():
         @pl.when(has_up)
@@ -525,10 +529,11 @@
             apply_up(0, v)
         product = jnp.dot(app_up[0], dn[0], preferred_element_type=F32)
         for a in range(3):
-            store(red_early, 6 + a, product[a * modes : (a + 1) * modes])
+            store(red_direct, a, product[a * modes : (a + 1) * modes])
 
     moved, done, arrived = set(), set(), set()
     started = False
+    handed = []
     for at, t in enumerate(order):
         await_chunks(1, [t], [t])
         arrived.add(t)
@@ -540,12 +545,19 @@
                 side_copy(1, 1).start()
 
         add_next(t, at == 0)
+        if at == 0:
+            self_sum.receive()
+            self_sum.send()
+            early_sum.receive()
+            early_sum.send()
         if at == 1:
             self_sum.receive()
             self_sum.send()
         if at == 2:
             finish_direct()
-            early_sum.send()
+            direct_sum.send()
+            early_sum.receive()
+            handed.append(hand_over(early_sum, 0, early_sem))
 
             @pl.when(has_up)
             def _():
@@ -554,20 +566,18 @@
 
         if at == 3:
             self_sum.receive()
-            early_sum.receive()
-            early_sum.send()
+            direct_sum.receive()
+            direct_sum.send()
         if at == tiles - 1:
-            early_sum.receive()
-            handed = hand_over()
-            handed.start()
-            for a in range(3):
-                for c in range(2):
-                    first = a * 2 * modes + c * modes
-                    store(red_next, 3 * c + a, acc_next[first : first + modes, :])
+            for c in range(2):
+                for a in range(3):
+                    store(red_next, 3 * c + a, acc_next[c, a * modes : (a + 1) * modes, :])
             next_sum = Halving(red_next, in_next, next_sem, bits)
             next_sum.send()
+            direct_sum.receive()
+            handed.append(hand_over(direct_sum, 6, direct_sem))
         if at >= 2:
-            blocks, ready = schedule(arrived, True, moved, done)
+            blocks, ready = schedule(arrived, moved, done)
             for u in blocks:
                 transposed(up.at[1], up_t.at[1], u)
             for v in ready:
@@ -646,7 +656,8 @@
         values = [red_self[self_sum.base, 3 * at + a].astype(F32) for a in range(3)]
         account(values, self_sum.base * share, share, 2 + c, 2 + b, None, c == b)
 
-    handed.wait_recv()
+    for copy in handed:
+        copy.wait_recv()
     next_sum.receive()
     spot_row = next_sum.base * part
     for c in range(2):
@@ -679,8 +690,8 @@
     def final_copy(delta, side, slab):
         slot = (1 - delta) * owners + rank
         return pltpu.make_async_remote_copy(
-            src_ref=given.at[2 * (delta + 1) + side],
-            dst_ref=taken.at[slot],
+            src_ref=packed.at[2 * (delta + 1) + side, pl.ds(0, 1)],
+            dst_ref=taken.at[slot, pl.ds(0, 1)],
             send_sem=fin_sem.at[0, (delta + 1) * owners + side * groups + slab],
             recv_sem=fin_sem.at[1, slot],
             device_id=(2 * (s + delta) + side, slab),
@@ -690,8 +701,8 @@
     def final_wait(delta, side, slab):
         slot = (delta + 1) * owners + side * groups + slab
         return pltpu.make_async_remote_copy(
-            src_ref=given.at[0],
-            dst_ref=taken.at[slot],
+            src_ref=packed.at[0, pl.ds(0, 1)],
+            dst_ref=taken.at[slot, pl.ds(0, 1)],
             send_sem=fin_sem.at[0, slot],
             recv_sem=fin_sem.at[1, slot],
             device_id=(2 * (s + delta) + side, slab),
@@ -708,17 +719,19 @@
                         condition = valid
                     pl.when(condition)(functools.partial(action, delta, side, slab))
 
+    packed[:, 0:1, :] = jnp.sum(given[...], axis=1, keepdims=True)
     for_all(lambda *at: final_copy(*at).start())
-    taken[owners + rank] = given[2 + y]
+    taken[owners + rank, 0:1] = packed[2 + y, 0:1]
     for_all(lambda *at: final_wait(*at).wait_recv())
-    total = jnp.sum(jnp.sum(taken[...], axis=0), axis=0, keepdims=True)
+    total = jnp.sum(taken[:, 0:1, :], axis=0)
     own_freq = frequency(mode)
     out_ref[...] = total / (own_freq * own_freq)
 
     for_all(lambda *at: final_copy(*at).wait_send())
-    for copy in self_sum.copies + early_sum.copies + next_sum.copies + skip_sum.copies:
-        copy.wait_send()
-    for copy in last_copies + [handed]:
+    for group in (self_sum, early_sum, direct_sum, next_sum, skip_sum):
+        for copy in group.copies:
+            copy.wait_send()
+    for copy in last_copies + handed:
         copy.wait_send()
     y_edge().wait_send()
     outer_edge().wait_send()
@@ -766,7 +779,7 @@
             pltpu.VMEM((2, padded, modes), BF16),
             pltpu.VMEM((2, padded, modes), BF16),
             pltpu.VMEM((2, rows, modes), BF16),
-            pltpu.VMEM((2 * modes, padded), BF16),
+            pltpu.VMEM((2, modes, padded), BF16),
             pltpu.VMEM((2, modes, padded), BF16),
             pltpu.VMEM((27, SLOTS, rows // 3), F32),
             pltpu.VMEM((SLOTS, rows // 3), jnp.int32),
@@ -778,15 +791,17 @@
             pltpu.VMEM((TILE, TILE), BF16),
             pltpu.VMEM((tiles, PERIOD, WIDE), BF16),
             pltpu.VMEM((3 * SLOTS * PERIOD + 16 * SLOTS, WIDE), BF16),
-            pltpu.VMEM((6 * modes, rows), BF16),
             pltpu.VMEM((2, 3 * modes, rows), BF16),
-            pltpu.VMEM((6 * modes, modes), F32),
+            pltpu.VMEM((2, 3 * modes, rows), BF16),
+            pltpu.VMEM((2, 3 * modes, modes), F32),
             pltpu.VMEM((3 * modes, modes), F32),
             pltpu.VMEM((3 * modes, modes), F32),
             pltpu.VMEM((owners, 9, share, modes), BF16),
             pltpu.VMEM((owners - 1, 9, share, modes), BF16),
-            pltpu.VMEM((groups, 9, part, modes), BF16),
-            pltpu.VMEM((groups - 1, 9, part, modes), BF16),
+            pltpu.VMEM((groups, 6, part, modes), BF16),
+            pltpu.VMEM((groups - 1, 6, part, modes), BF16),
+            pltpu.VMEM((groups, 3, part, modes), BF16),
+            pltpu.VMEM((groups - 1, 3, part, modes), BF16),
             pltpu.VMEM((9, part, modes), BF16),
             pltpu.VMEM((groups, 6, part, modes), BF16),
             pltpu.VMEM((groups - 1, 6, part, modes), BF16),
@@ -794,12 +809,14 @@
             pltpu.VMEM((groups - 1, 6, part, modes), BF16),
             pltpu.VMEM((3, 3, share, modes), BF16),
             pltpu.VMEM((6, 8, modes), F32),
+            pltpu.VMEM((6, 8, modes), F32),
             pltpu.VMEM((3 * owners, 8, modes), F32),
             dma((4,)),
             dma((2, tiles)),
             dma((2, 2, 2, tiles)),
             dma((2, 3)),
             dma((2, 2, 2)),
+            dma((2, levels + 1)),
             dma((2, levels + 1)),
             dma((2, levels + 1)),
             dma((2, levels)),

time: 48.6 us -> 48.5 us (level)
  no operation moved by 1% of the time
where the time goes in v2:
time: 48.5 us; the launch traced here: 48.3 us
  Pallas kernels  47.1 us (97%)
  other arithmetic  1.19 us (2%)
    pallas_call x1, Pallas kernels, local(): pl.pallas_call(functools.partial(kernel, sizes), out_shape=jax.ShapeDtype...  47.1 us
    mul x1, other arithmetic, local(): return result.reshape(modes) * (math.pi / 3.0)  1.19 us

profile of v2, /device:TPU:0, one launch (start us, length us, event | category | flops | bytes accessed | tf_op | source)
XLA Modules:
  0.0 48.3 jit_solution(11506140947765098432)
XLA Ops:
  0.0 47.1 %diffusivity.1 = f32[1,128]{1,0:T(1,128)} custom-call(bf16[3840,128]{1,0:T(8,128)(2,1)} %vec.1, f32[27,4,1280]{2,1,0:T(4,128)} %bitcast.6, s32[4,1280]{1,0:T(4,128)} %neighbours.1, f32[8,128]{1,0:T(8,128)} %bitcast.7), custom_call_target="tpu_custom_call" | custom-call | tf_op jit(solution)/shard_map/diffusivity/pallas_call | solution.py:773
  47.1 1.2 %multiply_bitcast_fusion = f32[128]{0:T(128)} fusion(f32[1,128]{1,0:T(1,128)} %diffusivity.1), kind=kLoop, calls=%fused_computation | loop fusion | flops 128 | bytes 1024 | tf_op jit(solution)/shard_map/mul | solution.py:832

commit v3 on v2

--- a/solution.py
+++ b/solution.py
@@ -406,27 +406,49 @@
         side_copy(0, 0).start()
         side_copy(0, 1).start()
 
+    moved, done, arrived = set(), set(), set(order[:2])
+
+    def own_step():
+        blocks, ready = schedule(arrived, moved, done)
+        for u in blocks:
+            transposed(own.at[other], own_t.at[other], u)
+        for v in ready:
+            apply_own(other, v)
+
     await_chunks(0, order[2:3], [])
     transposed(up.at[0], up_t.at[0], 1)
     forward(order[2])
+    arrived.add(order[2])
+    y_edge().wait_recv()
+    across_edge().wait_recv()
+    own_step()
     await_chunks(0, order[3:4], [])
     transposed(up.at[0], up_t.at[0], 2)
     apply_up(0, 1)
     forward(order[3])
+    arrived.add(order[3])
+    own_step()
     await_chunks(0, order[4:], order)
     for u in range(3, tiles):
         transposed(up.at[0], up_t.at[0], u)
     for v in range(2, tiles - 1):
         apply_up(0, v)
-    forward(order[4])
-    for t in order[5:]:
+
+    def store(buffer, index, piece):
+        count = buffer.shape[0]
+        buffer[:, index] = piece.astype(BF16).reshape(count, modes // count, modes)
+
+    def early(c):
+        product = jnp.dot(app_own[c], up[0, EDGE : EDGE + rows, :], preferred_element_type=F32)
+        for a in range(3):
+            store(red_early, 3 * c + a, product[a * modes : (a + 1) * modes])
+
+    early(y)
+    for t in order[4:]:
         forward(t)
-    y_edge().wait_recv()
-    across_edge().wait_recv()
-    for u in range(tiles + 1):
-        transposed(own.at[other], own_t.at[other], u)
-    for v in range(tiles):
-        apply_own(other, v)
+        arrived.add(t)
+        own_step()
+    early(other)
 
     bits = []
     bit = 1
@@ -435,6 +457,16 @@
         bits.append((side, (mode, atom + bit * (1 - 2 * side))))
         bit *= 2
     mate_bit = (y, (mate, atom))
+
+    def owner_of(slab):
+        place = 0
+        bit = 1
+        while bit < groups:
+            place = 2 * place + (slab // bit) % 2
+            bit *= 2
+        return place
+
+    mine = owner_of(atom)
 
     class Halving:
         def __init__(self, buffer, landing, sems, stages):
@@ -467,20 +499,17 @@
             self.base = self.keep
             self.stage += 1
 
-    def store(buffer, index, piece):
-        count = buffer.shape[0]
-        buffer[:, index] = piece.astype(BF16).reshape(count, modes // count, modes)
-
     early_sum = Halving(red_early, in_early, early_sem, bits)
+    early_sum.send()
+    own_main = jnp.concatenate([own[j, EDGE : EDGE + rows, :] for j in range(2)], axis=1)
     for c in range(2):
-        product = jnp.dot(app_own[c], up[0, EDGE : EDGE + rows, :], preferred_element_type=F32)
-        for a in range(3):
-            store(red_early, 3 * c + a, product[a * modes : (a + 1) * modes])
-    early_sum.send()
-    for at, (c, b) in enumerate(SELF_PAIRS):
-        product = jnp.dot(app_own[c], own[b, EDGE : EDGE + rows, :], preferred_element_type=F32)
-        for a in range(3):
-            store(red_self, 3 * at + a, product[a * modes : (a + 1) * modes])
+        blocks = own_main if c else own[0, EDGE : EDGE + rows, :]
+        product = jnp.dot(app_own[c], blocks, preferred_element_type=F32)
+        for at, (first, b) in enumerate(SELF_PAIRS):
+            if first == c:
+                for a in range(3):
+                    piece = product[a * modes : (a + 1) * modes, b * modes : (b + 1) * modes]
+                    store(red_self, 3 * at + a, piece)
     self_sum = Halving(red_self, in_self, self_sem, bits + [mate_bit])
     self_sum.send()
 
@@ -534,6 +563,15 @@
     moved, done, arrived = set(), set(), set()
     started = False
     handed = []
+    next_copies = []
+    skip_copies = []
+
+    def direct_copy(source, landing, sems, step):
+        target = (atom + step) % groups
+        return remote(
+            source.at[owner_of(target)], landing.at[step - 1], sems, (step - 1,), (mode, target)
+        )
+
     for at, t in enumerate(order):
         await_chunks(1, [t], [t])
         arrived.add(t)
@@ -572,8 +610,9 @@
             for c in range(2):
                 for a in range(3):
                     store(red_next, 3 * c + a, acc_next[c, a * modes : (a + 1) * modes, :])
-            next_sum = Halving(red_next, in_next, next_sem, bits)
-            next_sum.send()
+            for step in range(1, groups):
+                next_copies.append(direct_copy(red_next, in_next, next_sem, step))
+                next_copies[-1].start()
             direct_sum.receive()
             handed.append(hand_over(direct_sum, 6, direct_sem))
         if at >= 2:
@@ -589,40 +628,40 @@
         rows_a = slice(a * modes, (a + 1) * modes)
         store(red_skip, a, acc_skip[rows_a, :])
         store(red_skip, 3 + a, acc_mixed[rows_a, :])
-    skip_sum = Halving(red_skip, in_skip, skip_sem, bits[:-1])
-    for _ in bits[:-1]:
-        skip_sum.send()
-        next_sum.receive()
-        next_sum.send()
-        skip_sum.receive()
-    side, last = bits[-1]
-    keep = skip_sum.base + side
-    pass_on = skip_sum.base + 1 - side
+    keep = mine
     mine_rows = pl.ds(aligned(y * share), share)
     mate_rows = pl.ds(aligned(other * share), share)
-    last_copies = [
-        remote(
-            red_skip.at[pass_on, pl.ds(0, 3)],
-            in_skip.at[in_skip.shape[0] - 1, pl.ds(0, 3)],
-            mixed_sem,
-            (0,),
-            last,
-        ),
-        remote(
-            red_skip.at[pass_on, pl.ds(3, 3), mine_rows], in_mixed.at[0], mixed_sem, (1,), last
-        ),
-        remote(
-            red_skip.at[keep, pl.ds(3, 3), mate_rows], in_mixed.at[1], mixed_sem, (2,), mate_bit[1]
-        ),
-        remote(
-            red_skip.at[pass_on, pl.ds(3, 3), mate_rows],
-            in_mixed.at[2],
-            mixed_sem,
-            (3,),
-            (mate, last[1]),
-        ),
-    ]
-    for copy in last_copies:
+    for step in list(range(1, groups)) + [0]:
+        target = (atom + step) % groups
+        if step:
+            skip_copies.append(
+                remote(
+                    red_skip.at[owner_of(target), pl.ds(0, 3)],
+                    in_skip.at[step - 1],
+                    skip_sem,
+                    (step - 1,),
+                    (mode, target),
+                )
+            )
+            skip_copies.append(
+                remote(
+                    red_skip.at[owner_of(target), pl.ds(3, 3), mine_rows],
+                    in_mixed.at[step - 1],
+                    mixed_sem,
+                    (step - 1,),
+                    (mode, target),
+                )
+            )
+        skip_copies.append(
+            remote(
+                red_skip.at[owner_of(target), pl.ds(3, 3), mate_rows],
+                in_mixed.at[groups - 1 + step],
+                mixed_sem,
+                (groups - 1 + step,),
+                (mate, target),
+            )
+        )
+    for copy in skip_copies:
         copy.start()
 
     def frequency(block):
@@ -658,32 +697,35 @@
 
     for copy in handed:
         copy.wait_recv()
-    next_sum.receive()
-    spot_row = next_sum.base * part
+    for copy in next_copies:
+        copy.wait_recv()
     for c in range(2):
-        values = [
-            red_next[next_sum.base, 3 * c + a].astype(F32) + from_mate[3 * c + a].astype(F32)
-            for a in range(3)
-        ]
-        account(values, spot_row, part, 2 + c, 4 + other, has_up)
+        values = []
+        for a in range(3):
+            row = 3 * c + a
+            value = red_next[keep, row].astype(F32) + from_mate[row].astype(F32)
+            for step in range(1, groups):
+                value = value + in_next[step - 1, row].astype(F32)
+            values.append(value)
+        account(values, mine * part, part, 2 + c, 4 + other, has_up)
 
     both = jnp.logical_and(has_up, has_dn)
-    for copy in last_copies:
+    for copy in skip_copies:
         copy.wait_recv()
-    values = [
-        red_skip[keep, a].astype(F32)
-        + in_skip[in_skip.shape[0] - 1, a].astype(F32)
-        + from_mate[6 + a].astype(F32)
-        for a in range(3)
-    ]
-    account(values, keep * part, part, 4 + other, other, both)
+    values = []
+    for a in range(3):
+        value = red_skip[keep, a].astype(F32) + from_mate[6 + a].astype(F32)
+        for step in range(1, groups):
+            value = value + in_skip[step - 1, a].astype(F32)
+        values.append(value)
+    account(values, mine * part, part, 4 + other, other, both)
     values = []
     for a in range(3):
         value = red_skip[keep, 3 + a, mine_rows].astype(F32)
-        for i in range(3):
+        for i in range(owners - 1):
             value = value + in_mixed[i, a].astype(F32)
         values.append(value)
-    account(values, keep * part + y * share, share, 4, 1, both)
+    account(values, mine * part + y * share, share, 4, 1, both)
 
     rank = y * groups + atom
 
@@ -728,10 +770,10 @@
     out_ref[...] = total / (own_freq * own_freq)
 
     for_all(lambda *at: final_copy(*at).wait_send())
-    for group in (self_sum, early_sum, direct_sum, next_sum, skip_sum):
+    for group in (self_sum, early_sum, direct_sum):
         for copy in group.copies:
             copy.wait_send()
-    for copy in last_copies + handed:
+    for copy in next_copies + skip_copies + handed:
         copy.wait_send()
     y_edge().wait_send()
     outer_edge().wait_send()
@@ -806,8 +848,8 @@
             pltpu.VMEM((groups, 6, part, modes), BF16),
             pltpu.VMEM((groups - 1, 6, part, modes), BF16),
             pltpu.VMEM((groups, 6, part, modes), BF16),
-            pltpu.VMEM((groups - 1, 6, part, modes), BF16),
-            pltpu.VMEM((3, 3, share, modes), BF16),
+            pltpu.VMEM((groups - 1, 3, part, modes), BF16),
+            pltpu.VMEM((owners - 1, 3, share, modes), BF16),
             pltpu.VMEM((6, 8, modes), F32),
             pltpu.VMEM((6, 8, modes), F32),
             pltpu.VMEM((3 * owners, 8, modes), F32),
@@ -819,9 +861,9 @@
             dma((2, levels + 1)),
             dma((2, levels + 1)),
             dma((2, levels + 1)),
-            dma((2, levels)),
-            dma((2, levels)),
-            dma((2, 4)),
+            dma((2, groups - 1)),
+            dma((2, groups - 1)),
+            dma((2, owners - 1)),
             dma((2, 3 * owners)),
         ],
         compiler_params=pltpu.CompilerParams(

time: 48.5 us -> 46.4 us (0.957)
  Pallas kernels: 47.1 us -> 45 us
    pallas_call x1, Pallas kernels: 47.1 us -> 45 us  [local(): pl.pallas_call(functools.partial(kernel, sizes), out_shape=jax.ShapeDtype...]
where the time goes in v3:
time: 46.4 us; the launch traced here: 46.2 us
  Pallas kernels  45 us (97%)
  other arithmetic  1.19 us (3%)
    pallas_call x1, Pallas kernels, local(): pl.pallas_call(functools.partial(kernel, sizes), out_shape=jax.ShapeDtype...  45 us
    mul x1, other arithmetic, local(): return result.reshape(modes) * (math.pi / 3.0)  1.19 us

profile of v3, /device:TPU:0, one launch (start us, length us, event | category | flops | bytes accessed | tf_op | source)
XLA Modules:
  0.0 46.2 jit_solution(16158546175190586268)
XLA Ops:
  0.0 45.0 %diffusivity.1 = f32[1,128]{1,0:T(1,128)} custom-call(bf16[3840,128]{1,0:T(8,128)(2,1)} %vec.1, f32[27,4,1280]{2,1,0:T(4,128)} %bitcast.6, s32[4,1280]{1,0:T(4,128)} %neighbours.1, f32[8,128]{1,0:T(8,128)} %bitcast.7), custom_call_target="tpu_custom_call" | custom-call | tf_op jit(solution)/shard_map/diffusivity/pallas_call | solution.py:815
  45.0 1.2 %multiply_bitcast_fusion = f32[128]{0:T(128)} fusion(f32[1,128]{1,0:T(1,128)} %diffusivity.1), kind=kLoop, calls=%fused_computation | loop fusion | flops 128 | bytes 1024 | tf_op jit(solution)/shard_map/mul | solution.py:874

commit v4 on v3

--- a/solution.py
+++ b/solution.py
@@ -64,6 +64,7 @@
     acc_mixed,
     red_self,
     in_self,
+    self_mate,
     red_early,
     in_early,
     red_direct,
@@ -450,14 +451,6 @@
         own_step()
     early(other)
 
-    bits = []
-    bit = 1
-    while bit < groups:
-        side = (atom // bit) % 2
-        bits.append((side, (mode, atom + bit * (1 - 2 * side))))
-        bit *= 2
-    mate_bit = (y, (mate, atom))
-
     def owner_of(slab):
         place = 0
         bit = 1
@@ -467,39 +460,49 @@
         return place
 
     mine = owner_of(atom)
-
-    class Halving:
-        def __init__(self, buffer, landing, sems, stages):
-            self.buffer, self.landing, self.sems, self.stages = buffer, landing, sems, stages
-            self.base, self.size, self.at, self.stage = 0, buffer.shape[0], 0, 0
+    mine_rows = pl.ds(aligned(y * share), share)
+    mate_rows = pl.ds(aligned(other * share), share)
+
+    class Scatter:
+        def __init__(self, buffer, landing, sems):
+            self.buffer, self.landing, self.sems = buffer, landing, sems
             self.copies = []
 
         def send(self):
-            side, device = self.stages[self.stage]
-            self.size //= 2
-            self.keep = self.base + side * self.size
-            copy = remote(
-                self.buffer.at[pl.ds(self.base + (1 - side) * self.size, self.size)],
-                self.landing.at[pl.ds(self.at, self.size)],
-                self.sems,
-                (self.stage,),
-                device,
-            )
+            for step in range(1, groups):
+                target = (atom + step) % groups
+                copy = remote(
+                    self.buffer.at[owner_of(target)],
+                    self.landing.at[step - 1],
+                    self.sems,
+                    (step - 1,),
+                    (mode, target),
+                )
+                copy.start()
+                self.copies.append(copy)
+
+        def value(self, row):
+            total = self.buffer[mine, row].astype(F32)
+            for step in range(1, groups):
+                total = total + self.landing[step - 1, row].astype(F32)
+            return total
+
+        def await_all(self):
+            for copy in self.copies[: groups - 1]:
+                copy.wait_recv()
+
+        def hand_over(self, target, rows_sent):
+            self.await_all()
+            for row in range(self.buffer.shape[1]):
+                self.buffer[mine, row] = self.value(row).astype(BF16)
+            source = self.buffer.at[mine]
+            if rows_sent is not None:
+                source = source.at[:, rows_sent]
+            copy = remote(source, target, self.sems, (groups - 1,), (mate, atom))
             copy.start()
             self.copies.append(copy)
 
-        def receive(self):
-            self.copies[-1].wait_recv()
-            for i in range(self.size):
-                self.buffer[self.keep + i] = (
-                    self.buffer[self.keep + i].astype(F32)
-                    + self.landing[self.at + i].astype(F32)
-                ).astype(BF16)
-            self.at += self.size
-            self.base = self.keep
-            self.stage += 1
-
-    early_sum = Halving(red_early, in_early, early_sem, bits)
+    early_sum = Scatter(red_early, in_early, early_sem)
     early_sum.send()
     own_main = jnp.concatenate([own[j, EDGE : EDGE + rows, :] for j in range(2)], axis=1)
     for c in range(2):
@@ -510,7 +513,7 @@
                 for a in range(3):
                     piece = product[a * modes : (a + 1) * modes, b * modes : (b + 1) * modes]
                     store(red_self, 3 * at + a, piece)
-    self_sum = Halving(red_self, in_self, self_sem, bits + [mate_bit])
+    self_sum = Scatter(red_self, in_self, self_sem)
     self_sum.send()
 
     @pl.when(has_up)
@@ -527,25 +530,15 @@
             )
             acc_next[c] = term if start else acc_next[c] + term
 
-    def add_skip(t, start):
-        span = slice(t * WIDE, (t + 1) * WIDE)
+    def add_skip(first, last, start):
+        span = slice(first * WIDE, (last + 1) * WIDE)
         term = jnp.dot(app_up[1, :, span], dn[1, span, :], preferred_element_type=F32)
         acc_skip[...] = term if start else acc_skip[...] + term
         term = jnp.dot(app_up[y, :, span], dn[other, span, :], preferred_element_type=F32)
         acc_mixed[...] = term if start else acc_mixed[...] + term
 
-    direct_sum = Halving(red_direct, in_direct, direct_sem, bits)
-
-    def hand_over(source, place, sems):
-        copy = remote(
-            source.buffer.at[source.base],
-            from_mate.at[pl.ds(place, source.buffer.shape[1])],
-            sems,
-            (len(bits),),
-            mate_bit[1],
-        )
-        copy.start()
-        return copy
+    direct_sum = Scatter(red_direct, in_direct, direct_sem)
+    next_sum = Scatter(red_next, in_next, next_sem)
 
     def finish_direct():
         @pl.when(has_up)
@@ -562,16 +555,7 @@
 
     moved, done, arrived = set(), set(), set()
     started = False
-    handed = []
-    next_copies = []
     skip_copies = []
-
-    def direct_copy(source, landing, sems, step):
-        target = (atom + step) % groups
-        return remote(
-            source.at[owner_of(target)], landing.at[step - 1], sems, (step - 1,), (mode, target)
-        )
-
     for at, t in enumerate(order):
         await_chunks(1, [t], [t])
         arrived.add(t)
@@ -583,19 +567,11 @@
                 side_copy(1, 1).start()
 
         add_next(t, at == 0)
-        if at == 0:
-            self_sum.receive()
-            self_sum.send()
-            early_sum.receive()
-            early_sum.send()
         if at == 1:
-            self_sum.receive()
-            self_sum.send()
+            early_sum.hand_over(from_mate.at[pl.ds(0, 6)], None)
         if at == 2:
             finish_direct()
             direct_sum.send()
-            early_sum.receive()
-            handed.append(hand_over(early_sum, 0, early_sem))
 
             @pl.when(has_up)
             def _():
@@ -603,34 +579,31 @@
                 side_wait(1, 1).wait_recv()
 
         if at == 3:
-            self_sum.receive()
-            direct_sum.receive()
-            direct_sum.send()
+            self_sum.hand_over(self_mate, mate_rows)
         if at == tiles - 1:
             for c in range(2):
                 for a in range(3):
                     store(red_next, 3 * c + a, acc_next[c, a * modes : (a + 1) * modes, :])
-            for step in range(1, groups):
-                next_copies.append(direct_copy(red_next, in_next, next_sem, step))
-                next_copies[-1].start()
-            direct_sum.receive()
-            handed.append(hand_over(direct_sum, 6, direct_sem))
+            next_sum.send()
+            direct_sum.hand_over(from_mate.at[pl.ds(6, 3)], None)
         if at >= 2:
             blocks, ready = schedule(arrived, moved, done)
             for u in blocks:
                 transposed(up.at[1], up_t.at[1], u)
             for v in ready:
                 apply_up(1, v)
-                add_skip(v, not started)
+            runs = [v for v in ready if v - 1 not in ready]
+            for v in runs:
+                last = v
+                while last + 1 in ready:
+                    last += 1
+                add_skip(v, last, not started)
                 started = True
 
     for a in range(3):
         rows_a = slice(a * modes, (a + 1) * modes)
         store(red_skip, a, acc_skip[rows_a, :])
         store(red_skip, 3 + a, acc_mixed[rows_a, :])
-    keep = mine
-    mine_rows = pl.ds(aligned(y * share), share)
-    mate_rows = pl.ds(aligned(other * share), share)
     for step in list(range(1, groups)) + [0]:
         target = (atom + step) % groups
         if step:
@@ -691,22 +664,21 @@
             col_sum = jnp.sum(terms, axis=1, keepdims=True)
             given[c_index] = given[c_index] + folded(jnp.where(spot, col_sum, 0.0))
 
+    self_sum.copies[-1].wait_recv()
     for at, (c, b) in enumerate(SELF_PAIRS):
-        values = [red_self[self_sum.base, 3 * at + a].astype(F32) for a in range(3)]
-        account(values, self_sum.base * share, share, 2 + c, 2 + b, None, c == b)
-
-    for copy in handed:
-        copy.wait_recv()
-    for copy in next_copies:
-        copy.wait_recv()
+        values = [
+            red_self[mine, 3 * at + a, mine_rows].astype(F32) + self_mate[3 * at + a].astype(F32)
+            for a in range(3)
+        ]
+        account(values, mine * part + y * share, share, 2 + c, 2 + b, None, c == b)
+
+    early_sum.copies[-1].wait_recv()
+    direct_sum.copies[-1].wait_recv()
+    next_sum.await_all()
     for c in range(2):
-        values = []
-        for a in range(3):
-            row = 3 * c + a
-            value = red_next[keep, row].astype(F32) + from_mate[row].astype(F32)
-            for step in range(1, groups):
-                value = value + in_next[step - 1, row].astype(F32)
-            values.append(value)
+        values = [
+            next_sum.value(3 * c + a) + from_mate[3 * c + a].astype(F32) for a in range(3)
+        ]
         account(values, mine * part, part, 2 + c, 4 + other, has_up)
 
     both = jnp.logical_and(has_up, has_dn)
@@ -714,14 +686,14 @@
         copy.wait_recv()
     values = []
     for a in range(3):
-        value = red_skip[keep, a].astype(F32) + from_mate[6 + a].astype(F32)
+        value = red_skip[mine, a].astype(F32) + from_mate[6 + a].astype(F32)
         for step in range(1, groups):
             value = value + in_skip[step - 1, a].astype(F32)
         values.append(value)
     account(values, mine * part, part, 4 + other, other, both)
     values = []
     for a in range(3):
-        value = red_skip[keep, 3 + a, mine_rows].astype(F32)
+        value = red_skip[mine, 3 + a, mine_rows].astype(F32)
         for i in range(owners - 1):
             value = value + in_mixed[i, a].astype(F32)
         values.append(value)
@@ -770,10 +742,10 @@
     out_ref[...] = total / (own_freq * own_freq)
 
     for_all(lambda *at: final_copy(*at).wait_send())
-    for group in (self_sum, early_sum, direct_sum):
+    for group in (self_sum, early_sum, direct_sum, next_sum):
         for copy in group.copies:
             copy.wait_send()
-    for copy in next_copies + skip_copies + handed:
+    for copy in skip_copies:
         copy.wait_send()
     y_edge().wait_send()
     outer_edge().wait_send()
@@ -807,7 +779,6 @@
     owners = 2 * groups
     share = modes // owners
     part = modes // groups
-    levels = groups.bit_length() - 1
 
     blocks = couplings.transpose(1, 2, 3, 0, 4).reshape(27, SLOTS, rows_dev // 3)
     sizes = (blocks_all, groups, rows_dev, modes, half_width)
@@ -838,8 +809,9 @@
             pltpu.VMEM((2, 3 * modes, modes), F32),
             pltpu.VMEM((3 * modes, modes), F32),
             pltpu.VMEM((3 * modes, modes), F32),
-            pltpu.VMEM((owners, 9, share, modes), BF16),
-            pltpu.VMEM((owners - 1, 9, share, modes), BF16),
+            pltpu.VMEM((groups, 9, part, modes), BF16),
+            pltpu.VMEM((groups - 1, 9, part, modes), BF16),
+            pltpu.VMEM((9, share, modes), BF16),
             pltpu.VMEM((groups, 6, part, modes), BF16),
             pltpu.VMEM((groups - 1, 6, part, modes), BF16),
             pltpu.VMEM((groups, 3, part, modes), BF16),
@@ -858,9 +830,9 @@
             dma((2, 2, 2, tiles)),
             dma((2, 3)),
             dma((2, 2, 2)),
-            dma((2, levels + 1)),
-            dma((2, levels + 1)),
-            dma((2, levels + 1)),
+            dma((2, groups)),
+            dma((2, groups)),
+            dma((2, groups)),
             dma((2, groups - 1)),
             dma((2, groups - 1)),
             dma((2, owners - 1)),

time: 46.4 us -> 44.1 us (0.950)
  Pallas kernels: 45 us -> 42.7 us
    pallas_call x1, Pallas kernels: 45 us -> 42.7 us  [local(): pl.pallas_call(functools.partial(kernel, sizes), out_shape=jax.ShapeDtype...]
where the time goes in v4:
time: 44.1 us; the launch traced here: 43.9 us
  Pallas kernels  42.7 us (97%)
  other arithmetic  1.19 us (3%)
    pallas_call x1, Pallas kernels, local(): pl.pallas_call(functools.partial(kernel, sizes), out_shape=jax.ShapeDtype...  42.7 us
    mul x1, other arithmetic, local(): return result.reshape(modes) * (math.pi / 3.0)  1.19 us

profile of v4, /device:TPU:0, one launch (start us, length us, event | category | flops | bytes accessed | tf_op | source)
XLA Modules:
  0.0 43.9 jit_solution(9309225843672472139)
XLA Ops:
  0.0 42.7 %diffusivity.1 = f32[1,128]{1,0:T(1,128)} custom-call(bf16[3840,128]{1,0:T(8,128)(2,1)} %vec.1, f32[27,4,1280]{2,1,0:T(4,128)} %bitcast.6, s32[4,1280]{1,0:T(4,128)} %neighbours.1, f32[8,128]{1,0:T(8,128)} %bitcast.7), custom_call_target="tpu_custom_call" | custom-call | tf_op jit(solution)/shard_map/diffusivity/pallas_call | solution.py:786
  42.7 1.2 %multiply_bitcast_fusion = f32[128]{0:T(128)} fusion(f32[1,128]{1,0:T(1,128)} %diffusivity.1), kind=kLoop, calls=%fused_computation | loop fusion | flops 128 | bytes 1024 | tf_op jit(solution)/shard_map/mul | solution.py:846

commit v5 on v4

--- a/solution.py
+++ b/solution.py
@@ -606,25 +606,6 @@
         store(red_skip, 3 + a, acc_mixed[rows_a, :])
     for step in list(range(1, groups)) + [0]:
         target = (atom + step) % groups
-        if step:
-            skip_copies.append(
-                remote(
-                    red_skip.at[owner_of(target), pl.ds(0, 3)],
-                    in_skip.at[step - 1],
-                    skip_sem,
-                    (step - 1,),
-                    (mode, target),
-                )
-            )
-            skip_copies.append(
-                remote(
-                    red_skip.at[owner_of(target), pl.ds(3, 3), mine_rows],
-                    in_mixed.at[step - 1],
-                    mixed_sem,
-                    (step - 1,),
-                    (mode, target),
-                )
-            )
         skip_copies.append(
             remote(
                 red_skip.at[owner_of(target), pl.ds(3, 3), mate_rows],
@@ -632,6 +613,26 @@
                 mixed_sem,
                 (groups - 1 + step,),
                 (mate, target),
+            )
+        )
+    for step in range(1, groups):
+        target = (atom + step) % groups
+        skip_copies.append(
+            remote(
+                red_skip.at[owner_of(target), pl.ds(3, 3), mine_rows],
+                in_mixed.at[step - 1],
+                mixed_sem,
+                (step - 1,),
+                (mode, target),
+            )
+        )
+        skip_copies.append(
+            remote(
+                red_skip.at[owner_of(target), pl.ds(0, 3)],
+                in_skip.at[step - 1],
+                skip_sem,
+                (step - 1,),
+                (mode, target),
             )
         )
     for copy in skip_copies:
@@ -724,14 +725,16 @@
         )
 
     def for_all(action):
-        for delta, valid in ((0, None), (1, has_up), (-1, has_dn)):
-            for side in range(2):
-                for slab in range(groups):
+        for delta, valid in ((1, has_up), (-1, has_dn), (0, None)):
+            for turn in (1, 0):
+                for step in range(1, groups + 1):
+                    if delta == 0 and turn == 0 and step == groups:
+                        continue
+                    at = (delta, (y + turn) % 2, (atom + step) % groups)
                     if valid is None:
-                        condition = jnp.logical_or(side != y, slab != atom)
+                        action(*at)
                     else:
-                        condition = valid
-                    pl.when(condition)(functools.partial(action, delta, side, slab))
+                        pl.when(valid)(functools.partial(action, *at))
 
     packed[:, 0:1, :] = jnp.sum(given[...], axis=1, keepdims=True)
     for_all(lambda *at: final_copy(*at).start())
@@ -839,7 +842,7 @@
             dma((2, 3 * owners)),
         ],
         compiler_params=pltpu.CompilerParams(
-            collective_id=0, has_side_effects=True, vmem_limit_bytes=56 * 1024 * 1024
+            collective_id=0, has_side_effects=True, vmem_limit_bytes=55210 * 1024
         ),
         name="diffusivity",
     )(vectors, blocks, neighbours, frequency.reshape(blocks_all, modes))

time: 44.1 us -> 42.9 us (0.973)
  Pallas kernels: 42.7 us -> 41.5 us
  local copies, waits for them, and re-layouts: 0 us -> 0.69 us
  other arithmetic: 1.19 us -> 0.51 us
    pallas_call x1, Pallas kernels: 42.7 us -> 41.5 us  [local(): pl.pallas_call(functools.partial(kernel, sizes), out_shape=jax.ShapeDtype...]
    unnamed x0 -> x2, local copies, waits for them, and re-layouts: none -> 0.69 us
    mul x1, other arithmetic: 1.19 us -> 0.51 us  [local(): return result.reshape(modes) * (math.pi / 3.0)]
where the time goes in v5:
time: 42.9 us; the launch traced here: 42.7 us
  Pallas kernels  41.5 us (97%)
  local copies, waits for them, and re-layouts  0.69 us (2%)
  other arithmetic  0.51 us (1%)
    pallas_call x1, Pallas kernels, local(): pl.pallas_call(functools.partial(kernel, sizes), out_shape=jax.ShapeDtype...  41.5 us

profile of v5, /device:TPU:0, one launch (start us, length us, event | category | flops | bytes accessed | tf_op | source)
XLA Modules:
  0.0 42.7 jit_solution(5730481700371303002)
XLA Ops:
  0.0 0.0 copy-start
  0.0 0.7 %copy-done = f32[1024]{0:T(1024)S(1)} copy-done((f32[1024]{0:T(1024)S(1)}, f32[1024]{0:T(1024)}, u32[]{:S(2)}) %copy-start) | copy-done | bytes 4120
  0.7 41.5 %diffusivity.1 = f32[1,128]{1,0:T(1,128)S(1)} custom-call(bf16[3840,128]{1,0:T(8,128)(2,1)} %vec.1, f32[27,4,1280]{2,1,0:T(4,128)} %bitcast.7, s32[4,1280]{1,0:T(4,128)} %neighbours.1, f32[8,128]{1,0:T(8,128)S(1)} %bitcast.6), custom_call_target="tpu_custom_call" | custom-call | tf_op jit(solution)/shard_map/diffusivity/pallas_call | solution.py:789
  42.2 0.5 %multiply_bitcast_fusion = f32[128]{0:T(128)} fusion(f32[1,128]{1,0:T(1,128)S(1)} %diffusivity.1), kind=kLoop, calls=%fused_computation | loop fusion | flops 128 | bytes 1024 | tf_op jit(solution)/shard_map/mul | solution.py:849
Async XLA Ops:
  0.0 0.7 %copy-start = (f32[1024]{0:T(1024)S(1)}, f32[1024]{0:T(1024)}, u32[]{:S(2)}) copy-start(f32[1024]{0:T(1024)} %param.7) | copy-start | bytes 12292

commit v6 on v5

--- a/solution.py
+++ b/solution.py
@@ -567,24 +567,22 @@
                 side_copy(1, 1).start()
 
         add_next(t, at == 0)
-        if at == 1:
-            early_sum.hand_over(from_mate.at[pl.ds(0, 6)], None)
         if at == 2:
             finish_direct()
             direct_sum.send()
+            early_sum.hand_over(from_mate.at[pl.ds(0, 6)], None)
 
             @pl.when(has_up)
             def _():
                 side_wait(1, 0).wait_recv()
                 side_wait(1, 1).wait_recv()
 
-        if at == 3:
-            self_sum.hand_over(self_mate, mate_rows)
         if at == tiles - 1:
             for c in range(2):
                 for a in range(3):
                     store(red_next, 3 * c + a, acc_next[c, a * modes : (a + 1) * modes, :])
             next_sum.send()
+            self_sum.hand_over(self_mate, mate_rows)
             direct_sum.hand_over(from_mate.at[pl.ds(6, 3)], None)
         if at >= 2:
             blocks, ready = schedule(arrived, moved, done)

time: 42.9 us -> 42.6 us (level)
  no operation moved by 1% of the time
where the time goes in v6:
time: 42.6 us; the launch traced here: 42.5 us
  Pallas kernels  41.3 us (97%)
  local copies, waits for them, and re-layouts  0.69 us (2%)
  other arithmetic  0.51 us (1%)
    pallas_call x1, Pallas kernels, local(): pl.pallas_call(functools.partial(kernel, sizes), out_shape=jax.ShapeDtype...  41.3 us

profile of v6, /device:TPU:0, one launch (start us, length us, event | category | flops | bytes accessed | tf_op | source)
XLA Modules:
  0.0 42.5 jit_solution(15615279971428246511)
XLA Ops:
  0.0 0.0 copy-start
  0.0 0.7 %copy-done = f32[1024]{0:T(1024)S(1)} copy-done((f32[1024]{0:T(1024)S(1)}, f32[1024]{0:T(1024)}, u32[]{:S(2)}) %copy-start) | copy-done | bytes 4120
  0.7 41.3 %diffusivity.1 = f32[1,128]{1,0:T(1,128)S(1)} custom-call(bf16[3840,128]{1,0:T(8,128)(2,1)} %vec.1, f32[27,4,1280]{2,1,0:T(4,128)} %bitcast.7, s32[4,1280]{1,0:T(4,128)} %neighbours.1, f32[8,128]{1,0:T(8,128)S(1)} %bitcast.6), custom_call_target="tpu_custom_call" | custom-call | tf_op jit(solution)/shard_map/diffusivity/pallas_call | solution.py:787
  42.0 0.5 %multiply_bitcast_fusion = f32[128]{0:T(128)} fusion(f32[1,128]{1,0:T(1,128)S(1)} %diffusivity.1), kind=kLoop, calls=%fused_computation | loop fusion | flops 128 | bytes 1024 | tf_op jit(solution)/shard_map/mul | solution.py:847
Async XLA Ops:
  0.0 0.7 %copy-start = (f32[1024]{0:T(1024)S(1)}, f32[1024]{0:T(1024)}, u32[]{:S(2)}) copy-start(f32[1024]{0:T(1024)} %param.7) | copy-start | bytes 12292

commit v7 on v6

--- a/solution.py
+++ b/solution.py
@@ -737,12 +737,6 @@
     packed[:, 0:1, :] = jnp.sum(given[...], axis=1, keepdims=True)
     for_all(lambda *at: final_copy(*at).start())
     taken[owners + rank, 0:1] = packed[2 + y, 0:1]
-    for_all(lambda *at: final_wait(*at).wait_recv())
-    total = jnp.sum(taken[:, 0:1, :], axis=0)
-    own_freq = frequency(mode)
-    out_ref[...] = total / (own_freq * own_freq)
-
-    for_all(lambda *at: final_copy(*at).wait_send())
     for group in (self_sum, early_sum, direct_sum, next_sum):
         for copy in group.copies:
             copy.wait_send()
@@ -767,6 +761,13 @@
         for relay in range(2):
             for t in range(tiles):
                 z_copy(0, relay, t).wait_send()
+
+    for_all(lambda *at: final_wait(*at).wait_recv())
+    total = jnp.sum(taken[:, 0:1, :], axis=0)
+    own_freq = frequency(mode)
+    out_ref[...] = total / (own_freq * own_freq)
+
+    for_all(lambda *at: final_copy(*at).wait_send())
 
 
 def local(vectors, couplings, neighbours, frequency):

time: 42.6 us -> 42.6 us (level)
  no operation moved by 1% of the time
where the time goes in v7:
time: 42.6 us; the launch traced here: 42.4 us
  Pallas kernels  41.2 us (97%)
  local copies, waits for them, and re-layouts  0.69 us (2%)
  other arithmetic  0.51 us (1%)
    pallas_call x1, Pallas kernels, local(): pl.pallas_call(functools.partial(kernel, sizes), out_shape=jax.ShapeDtype...  41.2 us

profile of v7, /device:TPU:0, one launch (start us, length us, event | category | flops | bytes accessed | tf_op | source)
XLA Modules:
  0.0 42.4 jit_solution(15803776094051074594)
XLA Ops:
  0.0 0.0 copy-start
  0.0 0.7 %copy-done = f32[1024]{0:T(1024)S(1)} copy-done((f32[1024]{0:T(1024)S(1)}, f32[1024]{0:T(1024)}, u32[]{:S(2)}) %copy-start) | copy-done | bytes 4120
  0.7 41.2 %diffusivity.1 = f32[1,128]{1,0:T(1,128)S(1)} custom-call(bf16[3840,128]{1,0:T(8,128)(2,1)} %vec.1, f32[27,4,1280]{2,1,0:T(4,128)} %bitcast.7, s32[4,1280]{1,0:T(4,128)} %neighbours.1, f32[8,128]{1,0:T(8,128)S(1)} %bitcast.6), custom_call_target="tpu_custom_call" | custom-call | tf_op jit(solution)/shard_map/diffusivity/pallas_call | solution.py:788
  41.9 0.5 %multiply_bitcast_fusion = f32[128]{0:T(128)} fusion(f32[1,128]{1,0:T(1,128)S(1)} %diffusivity.1), kind=kLoop, calls=%fused_computation | loop fusion | flops 128 | bytes 1024 | tf_op jit(solution)/shard_map/mul | solution.py:848
Async XLA Ops:
  0.0 0.7 %copy-start = (f32[1024]{0:T(1024)S(1)}, f32[1024]{0:T(1024)}, u32[]{:S(2)}) copy-start(f32[1024]{0:T(1024)} %param.7) | copy-start | bytes 12292
